TPU v7x, 32 devices: a whole 2x2x4 slice. The times are simulated.
32 devices in a mesh: tm: 2 (over core), space: 16 (over z, y, x).
Axes of the slice: x: 2, y: 2, z: 4, core: 2. Of those that a mesh axis runs over, the one named last changes fastest.
Arguments:
- checkpoints: float32 [2, 5, 2048, 128], P('tm', None, 'space'), may hold values from -6 to 6
- sources: float32 [2, 5, 2048, 128], P(None, None, 'space'), may hold values from -3 to 3
- pitch: float32 [8], replicated, may hold values from -3.140625 to 3.140625
- metric: float32 [2048, 128], P('space'), may hold values from 0.5 to 2
- obj_weight: float32 [5, 2048, 128], P(None, 'space'), may hold values from 0.1 to 0.6
- adjoint_end: float32 [5, 2048, 128], P(None, 'space'), may hold values from -6 to 6
- lift: bfloat16 [5, 128, 128], replicated, may hold values from -0.5 to 0.5
- mixing: float32 [5, 5, 5], replicated, may hold values from -1.25 to 1.25
- faces: int32 [2048, 4], P('space'), may hold values from 0 to 191
- send_idx: int32 [16, 4, 16], P('space'), may hold values from 0 to 127
Outputs:
- adjoint_bounds: float32 [2, 5, 2048, 128], P('tm', None, 'space')
- pitch_grad: float32 [8], replicated
Inputs may be any that keep to these rules, and one draw needn't show every extreme that they name: `faces`: values below 128 name the subdomain's own blocks; value 128 + d * 16 + s names slot s of the blocks received from direction d. `send_idx`: entry [p, d, s] is a local block of subdomain p sent to subdomain p + o[d], o = (1, -1, 2, -2); blocks may repeat.
All inputs are finite; a program needn't handle non-finite values.
Results may differ from a plain program's by a relative error of at most 0.0035.
Values may be sent and summed in bfloat16 or wider, within the bound.
A program may use at most 64 MiB of HBM per device.

v0:
```python
import functools
import math

import jax
import jax.numpy as jnp
from jax import lax
from jax.experimental import pallas as pl
from jax.experimental.pallas import tpu as pltpu
from jax.sharding import PartitionSpec as P

OFFSETS = (1, -1, 2, -2)
STEP_SIZE = 0.5
F32 = jnp.float32
BF16 = jnp.bfloat16
MESH = pl.DeviceIdType.MESH


def dot(a, b):
    return jnp.dot(a, b, preferred_element_type=F32)


def window_kernel(
    dims,
    pitch_ref, mixing_ref, cp_hbm, src_hbm, metric_hbm, weight_hbm, end_hbm, lift_hbm, faces_hbm, send_hbm,
    out_ref, grad_ref,
    u_ref, lift_ref, faces_ref, send_ref, src_ref, metric_ref, weight_ref, a_ref, hand_ref, base_ref, dd_ref, wu_ref, lift_t, sq_ref,
    p_own, p_halo, pt_own, pt_halo, pick, pick_t, out_buf, in_buf, back_out, back_in, y_ref, yh_ref, z_ref,
    mixed_ref, g_ref, gw_ref, gh_ref, row_ref, rows_ref,
    load_sems, send_sems, recv_sems, bsend_sems, brecv_sems, hand_sems, factor_sems, gsend_sems, grecv_sems,
):
    comps, blocks, nodes, slots, halo, half, n_tm, n_space, norm = dims
    ghosts = 4 * halo
    faces_n = slots - 1
    wide = comps * nodes
    tm = lax.axis_index("tm")
    sp = lax.axis_index("space")
    n_dev = n_tm * n_space
    me = tm * n_space + sp
    lead = tm == n_tm - 1
    partner = (n_tm - 1 - tm, sp)
    segment = tm
    levels = half * n_tm

    loads = [
        pltpu.make_async_copy(send_hbm, send_ref, load_sems.at[5]),
        pltpu.make_async_copy(faces_hbm, faces_ref, load_sems.at[6]),
        pltpu.make_async_copy(cp_hbm.at[0], u_ref, load_sems.at[0]),
        pltpu.make_async_copy(lift_hbm, lift_ref, load_sems.at[7]),
        pltpu.make_async_copy(src_hbm, src_ref, load_sems.at[1]),
        pltpu.make_async_copy(metric_hbm, metric_ref, load_sems.at[2]),
        pltpu.make_async_copy(weight_hbm, weight_ref, load_sems.at[3]),
        pltpu.make_async_copy(end_hbm, a_ref, load_sems.at[4]),
    ]
    for load in loads:
        load.start()

    in_buf[...] = jnp.zeros_like(in_buf)
    back_in[...] = jnp.zeros_like(back_in)

    barrier = pltpu.get_barrier_semaphore()

    def greet(r, carry):
        other = lax.rem(me + r, n_dev)
        pl.semaphore_signal(
            barrier, inc=1, device_id=(other // n_space, lax.rem(other, n_space)), device_id_type=MESH
        )
        return carry

    lax.fori_loop(1, n_dev, greet, 0)

    for load in loads[:2]:
        load.wait()
    row_ids = lax.broadcasted_iota(jnp.int32, (blocks, blocks), 0)
    lane_ids = lax.broadcasted_iota(jnp.int32, (blocks, blocks), 1)
    face_cols = []
    for k in range(faces_n):
        turned = jnp.broadcast_to(faces_ref[k : k + 1, :], (blocks, blocks))
        col = jnp.transpose(turned.astype(F32)).astype(jnp.int32)
        face_cols.append(col)
        p_own[k * blocks : (k + 1) * blocks, :] = (col == lane_ids).astype(F32).astype(BF16)
        pt_own[k * blocks : (k + 1) * blocks, :] = (turned == row_ids).astype(F32).astype(BF16)
        hit = (turned[:ghosts] == row_ids[:ghosts] + blocks).astype(F32).astype(BF16)
        pt_halo[k * ghosts : (k + 1) * ghosts, :blocks] = hit
        pt_halo[k * ghosts : (k + 1) * ghosts, blocks:] = hit
    for pair in range(faces_n // 2):
        low = lane_ids < ghosts
        col = jnp.where(low, face_cols[2 * pair], face_cols[2 * pair + 1])
        want = jnp.where(low, lane_ids, lane_ids - ghosts) + blocks
        p_halo[:, pair * 2 * ghosts : (pair + 1) * 2 * ghosts] = (col == want).astype(F32).astype(BF16)
    wanted = jnp.concatenate(
        [send_ref[0, d : d + 1, :] for d in range(4)] + [jnp.full((1, blocks - ghosts), -1, jnp.int32)], axis=1
    )
    spread = jnp.broadcast_to(wanted, (blocks, blocks))
    pick_t[...] = (spread == row_ids).astype(F32).astype(BF16)[:, :ghosts]
    spread_t = jnp.transpose(spread.astype(F32)).astype(jnp.int32)
    pick[...] = (spread_t[:ghosts] == lane_ids[:ghosts]).astype(F32).astype(BF16)
    row_ref[...] = jnp.zeros_like(row_ref)
    loads[2].wait()

    def lanes(c):
        return slice(c * nodes, (c + 1) * nodes)

    def target(shift):
        return (tm, jnp.clip(sp + shift, 0, n_space - 1))

    def inside(shift):
        return (sp + shift >= 0) & (sp + shift < n_space)

    def forward_copy(n, d):
        rows = pl.ds(d * halo, halo)
        return pltpu.make_async_remote_copy(
            src_ref=out_buf.at[n, rows], dst_ref=in_buf.at[n, rows],
            send_sem=send_sems.at[n, d], recv_sem=recv_sems.at[n, d],
            device_id=target(OFFSETS[d]), device_id_type=MESH,
        )

    def backward_copy(n, d):
        rows = pl.ds(d * halo, halo)
        return pltpu.make_async_remote_copy(
            src_ref=back_out.at[n, rows], dst_ref=back_in.at[n, rows],
            send_sem=bsend_sems.at[n, d], recv_sem=brecv_sems.at[n, d],
            device_id=target(-OFFSETS[d]), device_id_type=MESH,
        )

    def coef(k, e, c):
        return mixing_ref[k, e, c]

    def turn_of(level):
        angle = jnp.full((8, nodes), pitch_ref[level], F32)
        return jnp.cos(angle)[0:1], jnp.sin(angle)[0:1]

    for c in range(comps):
        sq_ref[:, lanes(c)] = jnp.tanh(u_ref[c]).astype(BF16)
    out_buf[0] = dot(pick[...], sq_ref[...]).astype(BF16)
    pl.semaphore_wait(barrier, n_dev - 1)
    for d in range(4):
        @pl.when(inside(OFFSETS[d]))
        def _():
            forward_copy(0, d).start()

    chunk = 32
    for load in loads[3:]:
        load.wait()
    for k in range(slots):
        lift_t[:, k * nodes : (k + 1) * nodes] = jnp.transpose(lift_ref[k].astype(F32)).astype(BF16)

    def factor_copy(level, which):
        ref = (dd_ref, wu_ref)[which]
        return pltpu.make_async_remote_copy(
            src_ref=ref.at[level], dst_ref=ref.at[level], send_sem=factor_sems.at[0, which, level],
            recv_sem=factor_sems.at[1, which, level], device_id=partner, device_id_type=MESH,
        )

    def forward(n, carry):
        level = segment * half + n
        active = (n < half - 1) | lead

        @pl.when(active & (n > 0))
        def _():
            for c in range(comps):
                sq_ref[:, lanes(c)] = jnp.tanh(u_ref[c]).astype(BF16)
            out_buf[n] = dot(pick[...], sq_ref[...]).astype(BF16)
            for d in range(4):
                @pl.when(inside(OFFSETS[d]))
                def _():
                    forward_copy(n, d).start()

        keep = jnp.where(level > 0, 1.0, 0.0).astype(F32)
        for c in range(comps):
            state = u_ref[c]
            t = jnp.tanh(state)
            dd_ref[level, c] = STEP_SIZE * (1.0 - t * t)
            wu_ref[level, c] = (keep * weight_ref[c]) * state

        @pl.when(jnp.logical_not(lead))
        def _():
            factor_copy(level, 0).start()
            factor_copy(level, 1).start()

        @pl.when(active)
        def _():
            cosine, sine = turn_of(level)
            squashed = sq_ref[...]
            for k in range(slots):
                if k == 0:
                    got = squashed
                else:
                    got = dot(p_own[(k - 1) * blocks : k * blocks, :], squashed).astype(BF16)
                stacked = jnp.concatenate([got[:, lanes(c)] for c in range(comps)], axis=0)
                y_ref[k] = dot(stacked, lift_t[:, lanes(k)])

            def own_mix(r, carry):
                start = pl.multiple_of(r * chunk, chunk)
                metric_half = STEP_SIZE * metric_ref[pl.ds(start, chunk), :]
                sums = [None] * comps
                for k in range(slots):
                    for c in range(comps):
                        term = y_ref[k, pl.ds(c * blocks + start, chunk), :]
                        for e in range(comps):
                            add = coef(k, e, c) * term
                            sums[e] = add if sums[e] is None else sums[e] + add
                for e in range(comps):
                    rows = pl.ds(start, chunk)
                    forcing = cosine * src_ref[0, e, rows, :] + sine * src_ref[1, e, rows, :]
                    base_ref[e, rows, :] = u_ref[e, rows, :] + STEP_SIZE * forcing - metric_half * sums[e]
                return carry

            lax.fori_loop(0, blocks // chunk, own_mix, 0)

            for d in range(4):
                @pl.when(inside(-OFFSETS[d]))
                def _():
                    forward_copy(n, d).wait_recv()

            ghost = in_buf[n]
            stacked = jnp.concatenate([ghost[:, lanes(c)] for c in range(comps)], axis=0)
            yh_ref[...] = dot(stacked, lift_t[:, nodes:])
            for k in range(1, slots):
                for part in range(ghosts // chunk):
                    for e in range(comps):
                        total = None
                        for c in range(comps):
                            at = c * ghosts + part * chunk
                            add = coef(k, e, c) * yh_ref[at : at + chunk, lanes(k - 1)]
                            total = add if total is None else total + add
                        at = (k - 1) * ghosts + part * chunk
                        z_ref[at : at + chunk, lanes(e)] = total.astype(BF16)
            more = dot(p_halo[...], z_ref[...])
            half_metric = STEP_SIZE * metric_ref[...]
            for e in range(comps):
                u_ref[e] = base_ref[e] - half_metric * more[:, lanes(e)]
            for d in range(4):
                @pl.when(inside(OFFSETS[d]))
                def _():
                    forward_copy(n, d).wait_send()

        return carry

    lax.fori_loop(0, half, forward, 0)

    def hand_copy():
        return pltpu.make_async_remote_copy(
            src_ref=a_ref, dst_ref=out_ref.at[0], send_sem=hand_sems.at[0], recv_sem=hand_sems.at[1],
            device_id=partner, device_id_type=MESH,
        )

    def keep_copy():
        return pltpu.make_async_copy(hand_ref, out_ref.at[0], hand_sems.at[2])

    def grad_copy(source, other):
        return pltpu.make_async_remote_copy(
            src_ref=row_ref, dst_ref=rows_ref.at[source], send_sem=gsend_sems.at[other],
            recv_sem=grecv_sems.at[source], device_id=(other // n_space, lax.rem(other, n_space)),
            device_id_type=MESH,
        )

    def backward(j, carry):
        level = levels - 1 - j
        n = level

        for e in range(comps):
            w = metric_ref[...] * a_ref[e]
            high = w.astype(BF16)
            sq_ref[:, lanes(e)] = high
            mixed_ref[0, :, lanes(e)] = (w - high.astype(F32)).astype(BF16)
        gw_ref[...] = dot(pt_halo[...], jnp.concatenate([sq_ref[...], mixed_ref[0]], axis=0))
        for k in range(1, slots):
            for part in range(ghosts // chunk):
                at = (k - 1) * ghosts + part * chunk
                for c in range(comps):
                    total = None
                    for e in range(comps):
                        add = coef(k, e, c) * gw_ref[at : at + chunk, lanes(e)]
                        total = add if total is None else total + add
                    to = c * ghosts + part * chunk
                    gh_ref[to : to + chunk, lanes(k - 1)] = total.astype(BF16)
        lifted = dot(gh_ref[...], lift_ref[1:].reshape(faces_n * nodes, nodes)).astype(BF16)
        for c in range(comps):
            back_out[n, :, lanes(c)] = lifted[c * ghosts : (c + 1) * ghosts]
        for d in range(4):
            @pl.when(inside(-OFFSETS[d]))
            def _():
                backward_copy(n, d).start()

        @pl.when(level < half)
        def _():
            factor_copy(level, 0).wait_recv()
            factor_copy(level, 1).wait_recv()

        cosine, sine = turn_of(level)
        sums = None
        for e in range(comps):
            part = a_ref[e] * (cosine * src_ref[1, e] - sine * src_ref[0, e])
            sums = part if sums is None else sums + part
        value = jnp.sum(jnp.sum(sums, axis=0, keepdims=True), axis=1, keepdims=True) * (STEP_SIZE / norm)
        spots = lax.broadcasted_iota(jnp.int32, (1, nodes), 1)
        row_ref[...] = row_ref[...] + jnp.where(spots == level, value, 0.0)

        @pl.when(n == 0)
        def _():
            def tell(r, carry):
                grad_copy(sp, lax.rem(me + r, n_dev)).start()
                return carry

            lax.fori_loop(1, n_dev, tell, 0)

        def own_mix(r, carry):
            start = pl.multiple_of(r * chunk, chunk)
            rows = pl.ds(start, chunk)
            weighted = [metric_ref[rows, :] * a_ref[e, rows, :] for e in range(comps)]
            for k in range(slots):
                for c in range(comps):
                    total = None
                    for e in range(comps):
                        add = coef(k, e, c) * weighted[e]
                        total = add if total is None else total + add
                    mixed_ref[k, rows, lanes(c)] = total.astype(BF16)
            return carry

        lax.fori_loop(0, blocks // chunk, own_mix, 0)
        for k in range(slots):
            if k == 0:
                got = mixed_ref[0]
            else:
                got = dot(pt_own[(k - 1) * blocks : k * blocks, :], mixed_ref[k]).astype(BF16)
            for c in range(comps):
                g_ref[c * blocks : (c + 1) * blocks, lanes(k)] = got[:, lanes(c)]
        pushed = dot(g_ref[...], lift_ref[...].reshape(slots * nodes, nodes))
        for c in range(comps):
            base_ref[c] = a_ref[c] + wu_ref[n, c] - dd_ref[n, c] * pushed[c * blocks : (c + 1) * blocks]

        for d in range(4):
            @pl.when(inside(OFFSETS[d]))
            def _():
                backward_copy(n, d).wait_recv()

        more = dot(pick_t[...], back_in[n])
        for c in range(comps):
            a_ref[c] = base_ref[c] - dd_ref[n, c] * more[:, lanes(c)]
        for d in range(4):
            @pl.when(inside(-OFFSETS[d]))
            def _():
                backward_copy(n, d).wait_send()

        @pl.when(level == half)
        def _():
            for c in range(comps):
                hand_ref[c] = a_ref[c]
            keep_copy().start()

        return carry

    @pl.when(lead)
    def _():
        for c in range(comps):
            a_ref[c] = a_ref[c] + weight_ref[c] * u_ref[c]
        lax.fori_loop(0, levels, backward, 0)
        hand_copy().start()
        rows_ref[sp] = row_ref[...]

        def settle(r, carry):
            other = lax.rem(sp + r, n_space)
            grad_copy(other, me).wait_recv()
            return carry

        lax.fori_loop(1, n_space, settle, 0)

    @pl.when(jnp.logical_not(lead))
    def _():
        def settle(r, carry):
            grad_copy(r, me).wait_recv()
            return carry

        lax.fori_loop(0, n_space, settle, 0)

    grad_ref[...] = jnp.sum(rows_ref[...], axis=0)[0, : grad_ref.shape[0]]

    @pl.when(lead)
    def _():
        hand_copy().wait_send()
        keep_copy().wait()

        def sent(r, carry):
            grad_copy(sp, lax.rem(me + r, n_dev)).wait_send()
            return carry

        lax.fori_loop(1, n_dev, sent, 0)

    @pl.when(jnp.logical_not(lead))
    def _():
        hand_copy().wait_recv()
        for level in range(half):
            factor_copy(level, 0).wait_send()
            factor_copy(level, 1).wait_send()


def shards(
    checkpoints, sources, pitch, metric, obj_weight, adjoint_end, lift, mixing, faces, send_idx
):
    comps = sources.shape[1]
    blocks, nodes = metric.shape
    slots = lift.shape[0]
    halo = send_idx.shape[2]
    n_tm = lax.axis_size("tm")
    n_space = lax.axis_size("space")
    levels = pitch.shape[0]
    half = levels // n_tm
    ghosts = 4 * halo
    norm = math.sqrt(comps * nodes * blocks * n_space)
    wide = comps * nodes
    field = (comps, blocks, nodes)
    vmem = pl.BlockSpec(memory_space=pltpu.VMEM)
    smem = pl.BlockSpec(memory_space=pltpu.SMEM)
    anym = pl.BlockSpec(memory_space=pl.ANY)
    dma = pltpu.SemaphoreType.DMA
    n_dev = n_tm * n_space
    dims = (comps, blocks, nodes, slots, halo, half, n_tm, n_space, norm)
    bounds, grad = pl.pallas_call(
        functools.partial(window_kernel, dims),
        out_shape=(
            jax.ShapeDtypeStruct((1, *field), F32),
            jax.ShapeDtypeStruct((levels,), F32),
        ),
        in_specs=[smem, smem] + [anym] * 8,
        out_specs=(anym, vmem),
        scratch_shapes=[
            pltpu.VMEM(field, F32),
            pltpu.VMEM(lift.shape, BF16),
            pltpu.VMEM(faces.shape[::-1], jnp.int32),
            pltpu.VMEM(send_idx.shape, jnp.int32),
            pltpu.VMEM((2, *field), F32),
            pltpu.VMEM((blocks, nodes), F32),
            pltpu.VMEM(field, F32),
            pltpu.VMEM(field, F32),
            pltpu.VMEM(field, F32),
            pltpu.VMEM(field, F32),
            pltpu.VMEM((levels, *field), F32),
            pltpu.VMEM((levels, *field), F32),
            pltpu.VMEM((nodes, slots * nodes), BF16),
            pltpu.VMEM((blocks, wide), BF16),
            pltpu.VMEM(((slots - 1) * blocks, blocks), BF16),
            pltpu.VMEM((blocks, (slots - 1) * ghosts), BF16),
            pltpu.VMEM(((slots - 1) * blocks, blocks), BF16),
            pltpu.VMEM(((slots - 1) * ghosts, 2 * blocks), BF16),
            pltpu.VMEM((ghosts, blocks), BF16),
            pltpu.VMEM((blocks, ghosts), BF16),
            pltpu.VMEM((half, ghosts, wide), BF16),
            pltpu.VMEM((half, ghosts, wide), BF16),
            pltpu.VMEM((levels, ghosts, wide), BF16),
            pltpu.VMEM((levels, ghosts, wide), BF16),
            pltpu.VMEM((slots, comps * blocks, nodes), F32),
            pltpu.VMEM((comps * ghosts, (slots - 1) * nodes), F32),
            pltpu.VMEM(((slots - 1) * ghosts, wide), BF16),
            pltpu.VMEM((slots, blocks, wide), BF16),
            pltpu.VMEM((comps * blocks, slots * nodes), BF16),
            pltpu.VMEM(((slots - 1) * ghosts, wide), F32),
            pltpu.VMEM((comps * ghosts, (slots - 1) * nodes), BF16),
            pltpu.VMEM((1, nodes), F32),
            pltpu.VMEM((n_space, 1, nodes), F32),
            dma((8,)),
            dma((half, 4)),
            dma((half, 4)),
            dma((levels, 4)),
            dma((levels, 4)),
            dma((3,)),
            dma((2, 2, half)),
            dma((n_dev,)),
            dma((n_space,)),
        ],
        compiler_params=pltpu.CompilerParams(
            collective_id=0, has_side_effects=True, vmem_limit_bytes=60 * 1024 * 1024
        ),
        name="window",
    )(pitch, mixing, checkpoints, sources, metric, obj_weight, adjoint_end, lift, faces.T, send_idx)
    return bounds, grad


def solution(mesh):
    placed = (
        P("tm", None, "space", None),
        P(None, None, "space", None),
        P(),
        P("space", None),
        P(None, "space", None),
        P(None, "space", None),
        P(),
        P(),
        P("space", None),
        P("space", None, None),
    )
    return jax.shard_map(
        shards,
        mesh=mesh,
        in_specs=placed,
        out_specs=(P("tm", None, "space", None), P()),
        check_vma=False,
    )
```

profile of v0, /device:TPU:1, one launch (start us, length us, event | category | flops | bytes accessed | tf_op | source)
XLA Modules:
  0.0 57.2 jit_solution(21571065214977280)
XLA Ops:
  0.6 54.3 %window.1 = (f32[1,5,128,128]{3,2,1,0:T(8,128)}, f32[8]{0:T(128)}) custom-call(f32[8]{0:T(128)} %pitch_ref.1, f32[5,5,5]{2,1,0:T(8,128)} %mixing_ref.1, f32[1,5,128,128]{3,2,1,0:T(8,128)} %cp_hbm.1, f32[2,5,128,128]{3,2,1,0:T(8,128)} %src_hbm.1, f32[128,128]{1,0:T(8,128)} %metric_hbm.1, f32[5,128,128]{2,1,0:T(8,128)} %weight_hbm.1, f32[5,128,128]{2,1,0:T(8,128)} %end_hbm.1, ...), custom_call_target="tpu_custom_call" | custom-call | tf_op jit(solution)/shard_map/window/pallas_call | solution.py:418
  54.9 0.0 copy-start
  54.9 1.7 %copy.14 = f32[1,5,128,128]{3,2,1,0:T(8,128)} copy(f32[1,5,128,128]{3,2,1,0:T(8,128)} %get-tuple-element.4) | data formatting | bytes 655360
  56.7 0.0 copy-done
  56.7 0.5 copy.15
Async XLA Ops:
  54.9 1.7 %copy-start = (f32[8]{0:T(128)S(1)}, f32[8]{0:T(128)}, u32[]{:S(2)}) copy-start(f32[8]{0:T(128)} %get-tuple-element.5) | copy-start | bytes 100
where the time goes:
time: 57.5 us; the launch traced here: 57.2 us
  Pallas kernels  54.3 us (94%)
  local copies, waits for them, and re-layouts  2.23 us (4%)
  between operations  0.65 us (1%)
    pallas_call x1, Pallas kernels, shards(): pl.pallas_call(functools.partial(window_kernel, dims), out_shape=(jax.Sha...  54.3 us
    unnamed x4, local copies, waits for them, and re-layouts  2.23 us

commit v1 on v0

--- a/solution.py
+++ b/solution.py
@@ -26,7 +26,9 @@
     u_ref, lift_ref, faces_ref, send_ref, src_ref, metric_ref, weight_ref, a_ref, hand_ref, base_ref, dd_ref, wu_ref, lift_t, sq_ref,
     p_own, p_halo, pt_own, pt_halo, pick, pick_t, out_buf, in_buf, back_out, back_in, y_ref, yh_ref, z_ref,
     mixed_ref, g_ref, gw_ref, gh_ref, row_ref, rows_ref,
+    pick_t2, low_ref, wf_ref, et_out, et_in, mg_out, mg_in, dup_out, dup_in, last_ref,
     load_sems, send_sems, recv_sems, bsend_sems, brecv_sems, hand_sems, factor_sems, gsend_sems, grecv_sems,
+    table_sems, metric_sems, ghost_sems, dsend_sems, drecv_sems,
 ):
     comps, blocks, nodes, slots, halo, half, n_tm, n_space, norm = dims
     ghosts = 4 * halo
@@ -55,7 +57,13 @@
         load.start()
 
     in_buf[...] = jnp.zeros_like(in_buf)
-    back_in[...] = jnp.zeros_like(back_in)
+
+    @pl.when(lead)
+    def _():
+        back_in[...] = jnp.zeros_like(back_in)
+        et_in[...] = jnp.zeros_like(et_in)
+        mg_in[...] = jnp.zeros_like(mg_in)
+        dup_in[...] = jnp.zeros_like(dup_in)
 
     barrier = pltpu.get_barrier_semaphore()
 
@@ -92,6 +100,8 @@
     )
     spread = jnp.broadcast_to(wanted, (blocks, blocks))
     pick_t[...] = (spread == row_ids).astype(F32).astype(BF16)[:, :ghosts]
+    doubled = jnp.concatenate([wanted[:, :ghosts]] * 2, axis=1)
+    pick_t2[...] = (jnp.broadcast_to(doubled, (blocks, 2 * ghosts)) == row_ids).astype(F32).astype(BF16)
     spread_t = jnp.transpose(spread.astype(F32)).astype(jnp.int32)
     pick[...] = (spread_t[:ghosts] == lane_ids[:ghosts]).astype(F32).astype(BF16)
     row_ref[...] = jnp.zeros_like(row_ref)
@@ -109,10 +119,45 @@
     def forward_copy(n, d):
         rows = pl.ds(d * halo, halo)
         return pltpu.make_async_remote_copy(
-            src_ref=out_buf.at[n, rows], dst_ref=in_buf.at[n, rows],
+            src_ref=out_buf.at[n, rows], dst_ref=in_buf.at[segment * half + n, rows],
             send_sem=send_sems.at[n, d], recv_sem=recv_sems.at[n, d],
             device_id=target(OFFSETS[d]), device_id_type=MESH,
         )
+
+    def ghost_copy(n, d):
+        rows = pl.ds(d * halo, halo)
+        return pltpu.make_async_remote_copy(
+            src_ref=out_buf.at[n, rows], dst_ref=in_buf.at[n, rows],
+            send_sem=ghost_sems.at[0, n // 2, d], recv_sem=ghost_sems.at[1, n // 2, d],
+            device_id=(n_tm - 1, jnp.clip(sp + OFFSETS[d], 0, n_space - 1)), device_id_type=MESH,
+        )
+
+    def metric_copy(d):
+        rows = pl.ds(d * halo, halo)
+        return pltpu.make_async_remote_copy(
+            src_ref=mg_out.at[rows], dst_ref=mg_in.at[rows],
+            send_sem=metric_sems.at[0, d], recv_sem=metric_sems.at[1, d],
+            device_id=target(OFFSETS[d]), device_id_type=MESH,
+        )
+
+    def table_copy(d):
+        rows = pl.ds(d * faces_n * halo, faces_n * halo)
+        return pltpu.make_async_remote_copy(
+            src_ref=et_out.at[rows], dst_ref=et_in.at[rows],
+            send_sem=table_sems.at[0, d], recv_sem=table_sems.at[1, d],
+            device_id=target(-OFFSETS[d]), device_id_type=MESH,
+        )
+
+    def second_copy(slot, d, far):
+        rows = pl.ds(far * halo, halo)
+        return pltpu.make_async_remote_copy(
+            src_ref=dup_out.at[slot, rows], dst_ref=dup_in.at[slot, d, rows],
+            send_sem=dsend_sems.at[slot, 4 * d + far], recv_sem=drecv_sems.at[slot, 4 * d + far],
+            device_id=target(-OFFSETS[far] - OFFSETS[d]), device_id_type=MESH,
+        )
+
+    def second_pairs():
+        return [(d, far) for d in range(4) for far in range(4) if OFFSETS[d] + OFFSETS[far] != 0]
 
     def backward_copy(n, d):
         rows = pl.ds(d * halo, halo)
@@ -144,6 +189,28 @@
     for k in range(slots):
         lift_t[:, k * nodes : (k + 1) * nodes] = jnp.transpose(lift_ref[k].astype(F32)).astype(BF16)
 
+    @pl.when(lead)
+    def _():
+        four = jnp.concatenate([wanted[:, :ghosts]] * 4, axis=1)
+        ids = lax.broadcasted_iota(jnp.int32, (blocks, 4 * ghosts), 0)
+        picks = (jnp.broadcast_to(four, (blocks, 4 * ghosts)) == ids).astype(F32).astype(BF16)
+        table = dot(pt_halo[:, :blocks], picks)
+        part = lax.broadcasted_iota(jnp.int32, (halo, 4 * ghosts), 1) // ghosts
+        for d in range(4):
+            for k in range(faces_n):
+                piece = table[k * ghosts + d * halo : k * ghosts + (d + 1) * halo]
+                to = (d * faces_n + k) * halo
+                et_out[to : to + halo, :] = jnp.where(part == d, piece, 0.0).astype(BF16)
+        mg_out[...] = dot(pick[...], metric_ref[...].astype(BF16)).astype(BF16)
+        for d in range(4):
+            @pl.when(inside(OFFSETS[d]))
+            def _():
+                metric_copy(d).start()
+
+            @pl.when(inside(-OFFSETS[d]))
+            def _():
+                table_copy(d).start()
+
     def factor_copy(level, which):
         ref = (dd_ref, wu_ref)[which]
         return pltpu.make_async_remote_copy(
@@ -155,15 +222,19 @@
         level = segment * half + n
         active = (n < half - 1) | lead
 
-        @pl.when(active & (n > 0))
+        @pl.when(n > 0)
         def _():
             for c in range(comps):
                 sq_ref[:, lanes(c)] = jnp.tanh(u_ref[c]).astype(BF16)
             out_buf[n] = dot(pick[...], sq_ref[...]).astype(BF16)
             for d in range(4):
-                @pl.when(inside(OFFSETS[d]))
+                @pl.when(inside(OFFSETS[d]) & active)
                 def _():
                     forward_copy(n, d).start()
+
+                @pl.when(inside(OFFSETS[d]) & jnp.logical_not(lead) & (lax.rem(n, 2) == 1))
+                def _():
+                    ghost_copy(n, d).start()
 
         keep = jnp.where(level > 0, 1.0, 0.0).astype(F32)
         for c in range(comps):
@@ -212,7 +283,7 @@
                 def _():
                     forward_copy(n, d).wait_recv()
 
-            ghost = in_buf[n]
+            ghost = in_buf[level]
             stacked = jnp.concatenate([ghost[:, lanes(c)] for c in range(comps)], axis=0)
             yh_ref[...] = dot(stacked, lift_t[:, nodes:])
             for k in range(1, slots):
@@ -254,39 +325,59 @@
             device_id_type=MESH,
         )
 
-    def backward(j, carry):
-        level = levels - 1 - j
-        n = level
-
+    def mix_back(k, at, rows, to):
+        for c in range(comps):
+            total = None
+            for e in range(comps):
+                add = coef(k, e, c) * gw_ref[at : at + rows, lanes(e)]
+                total = add if total is None else total + add
+            gh_ref[c * ghosts + to : c * ghosts + to + rows, lanes(k - 1)] = total.astype(BF16)
+
+    def lift_back():
+        return dot(gh_ref[...], lift_ref[1:].reshape(faces_n * nodes, nodes))
+
+    def halo_part(ref, level, keep):
         for e in range(comps):
-            w = metric_ref[...] * a_ref[e]
+            w = metric_ref[...] * ref[e]
+            if keep:
+                wf_ref[e] = w
             high = w.astype(BF16)
             sq_ref[:, lanes(e)] = high
-            mixed_ref[0, :, lanes(e)] = (w - high.astype(F32)).astype(BF16)
-        gw_ref[...] = dot(pt_halo[...], jnp.concatenate([sq_ref[...], mixed_ref[0]], axis=0))
+            low_ref[:, lanes(e)] = (w - high.astype(F32)).astype(BF16)
+        gw_ref[...] = dot(pt_halo[...], jnp.concatenate([sq_ref[...], low_ref[...]], axis=0))
         for k in range(1, slots):
             for part in range(ghosts // chunk):
-                at = (k - 1) * ghosts + part * chunk
+                mix_back(k, (k - 1) * ghosts + part * chunk, chunk, part * chunk)
+        lifted = lift_back().astype(BF16)
+        for c in range(comps):
+            back_out[level, :, lanes(c)] = lifted[c * ghosts : (c + 1) * ghosts]
+        for d in range(4):
+            @pl.when(inside(-OFFSETS[d]))
+            def _():
+                backward_copy(level, d).start()
+
+    def own_part(level):
+        for k in range(slots):
+            for r in range(blocks // chunk):
+                rows = slice(r * chunk, (r + 1) * chunk)
+                weighted = [wf_ref[e, rows, :] for e in range(comps)]
                 for c in range(comps):
                     total = None
                     for e in range(comps):
-                        add = coef(k, e, c) * gw_ref[at : at + chunk, lanes(e)]
+                        add = coef(k, e, c) * weighted[e]
                         total = add if total is None else total + add
-                    to = c * ghosts + part * chunk
-                    gh_ref[to : to + chunk, lanes(k - 1)] = total.astype(BF16)
-        lifted = dot(gh_ref[...], lift_ref[1:].reshape(faces_n * nodes, nodes)).astype(BF16)
-        for c in range(comps):
-            back_out[n, :, lanes(c)] = lifted[c * ghosts : (c + 1) * ghosts]
-        for d in range(4):
-            @pl.when(inside(-OFFSETS[d]))
-            def _():
-                backward_copy(n, d).start()
-
-        @pl.when(level < half)
-        def _():
-            factor_copy(level, 0).wait_recv()
-            factor_copy(level, 1).wait_recv()
-
+                    mixed_ref[k, rows, lanes(c)] = total.astype(BF16)
+            if k == 0:
+                got = mixed_ref[0]
+            else:
+                got = dot(pt_own[(k - 1) * blocks : k * blocks, :], mixed_ref[k]).astype(BF16)
+            for c in range(comps):
+                g_ref[c * blocks : (c + 1) * blocks, lanes(k)] = got[:, lanes(c)]
+        pushed = dot(g_ref[...], lift_ref[...].reshape(slots * nodes, nodes))
+        for c in range(comps):
+            base_ref[c] = a_ref[c] + wu_ref[level, c] - dd_ref[level, c] * pushed[c * blocks : (c + 1) * blocks]
+
+    def add_grad(level):
         cosine, sine = turn_of(level)
         sums = None
         for e in range(comps):
@@ -296,7 +387,61 @@
         spots = lax.broadcasted_iota(jnp.int32, (1, nodes), 1)
         row_ref[...] = row_ref[...] + jnp.where(spots == level, value, 0.0)
 
-        @pl.when(n == 0)
+    def backward(j, carry):
+        high = levels - 1 - 2 * j
+        low = high - 1
+
+        halo_part(a_ref, high, True)
+
+        @pl.when(j == 0)
+        def _():
+            for d in range(4):
+                @pl.when(inside(-OFFSETS[d]))
+                def _():
+                    metric_copy(d).wait_recv()
+
+        @pl.when(high < half)
+        def _():
+            for d in range(4):
+                @pl.when(inside(-OFFSETS[d]))
+                def _():
+                    ghost_copy(high, d).wait_recv()
+
+            for which in range(2):
+                factor_copy(high, which).wait_recv()
+                factor_copy(low, which).wait_recv()
+
+        spread_metric = mg_in[...].astype(F32)
+        for c in range(comps):
+            t = in_buf[high, :, lanes(c)].astype(F32)
+            factor = spread_metric * (STEP_SIZE - STEP_SIZE * t * t)
+            dup_out[j, :, lanes(c)] = (factor * back_out[high, :, lanes(c)].astype(F32)).astype(BF16)
+        for d, far in second_pairs():
+            @pl.when(inside(-OFFSETS[far]) & inside(-OFFSETS[far] - OFFSETS[d]))
+            def _():
+                second_copy(j, d, far).start()
+        for far in range(4):
+            d = OFFSETS.index(-OFFSETS[far])
+            dup_in[j, d, far * halo : (far + 1) * halo, :] = dup_out[j, far * halo : (far + 1) * halo, :]
+
+        add_grad(high)
+        own_part(high)
+        halo_part(base_ref, low, False)
+
+        for d in range(4):
+            @pl.when(inside(OFFSETS[d]))
+            def _():
+                backward_copy(high, d).wait_recv()
+
+        more = dot(pick_t[...], back_in[high])
+        for c in range(comps):
+            state = base_ref[c] - dd_ref[high, c] * more[:, lanes(c)]
+            a_ref[c] = state
+            wf_ref[c] = metric_ref[...] * state
+
+        add_grad(low)
+
+        @pl.when(low == 0)
         def _():
             def tell(r, carry):
                 grad_copy(sp, lax.rem(me + r, n_dev)).start()
@@ -304,45 +449,54 @@
 
             lax.fori_loop(1, n_dev, tell, 0)
 
-        def own_mix(r, carry):
-            start = pl.multiple_of(r * chunk, chunk)
-            rows = pl.ds(start, chunk)
-            weighted = [metric_ref[rows, :] * a_ref[e, rows, :] for e in range(comps)]
-            for k in range(slots):
-                for c in range(comps):
-                    total = None
-                    for e in range(comps):
-                        add = coef(k, e, c) * weighted[e]
-                        total = add if total is None else total + add
-                    mixed_ref[k, rows, lanes(c)] = total.astype(BF16)
-            return carry
-
-        lax.fori_loop(0, blocks // chunk, own_mix, 0)
-        for k in range(slots):
-            if k == 0:
-                got = mixed_ref[0]
-            else:
-                got = dot(pt_own[(k - 1) * blocks : k * blocks, :], mixed_ref[k]).astype(BF16)
-            for c in range(comps):
-                g_ref[c * blocks : (c + 1) * blocks, lanes(k)] = got[:, lanes(c)]
-        pushed = dot(g_ref[...], lift_ref[...].reshape(slots * nodes, nodes))
-        for c in range(comps):
-            base_ref[c] = a_ref[c] + wu_ref[n, c] - dd_ref[n, c] * pushed[c * blocks : (c + 1) * blocks]
+        own_part(low)
+
+        @pl.when(j == 0)
+        def _():
+            for d in range(4):
+                @pl.when(inside(OFFSETS[d]))
+                def _():
+                    table_copy(d).wait_recv()
+                    metric_copy(d).wait_send()
+
+                @pl.when(inside(-OFFSETS[d]))
+                def _():
+                    table_copy(d).wait_send()
+
+        for d, far in second_pairs():
+            @pl.when(inside(OFFSETS[d]) & inside(OFFSETS[d] + OFFSETS[far]))
+            def _():
+                second_copy(j, d, far).wait_recv()
+
+        gw_ref[...] = dot(et_in[...], dup_in[j].reshape(4 * ghosts, wide))
+        for k in range(1, slots):
+            for d in range(4):
+                mix_back(k, (d * faces_n + k - 1) * halo, halo, d * halo)
+        lifted = lift_back()
+        for c in range(comps):
+            last_ref[ghosts:, lanes(c)] = (-lifted[c * ghosts : (c + 1) * ghosts]).astype(BF16)
+
+        for d, far in second_pairs():
+            @pl.when(inside(-OFFSETS[far]) & inside(-OFFSETS[far] - OFFSETS[d]))
+            def _():
+                second_copy(j, d, far).wait_send()
+        for d in range(4):
+            @pl.when(inside(-OFFSETS[d]))
+            def _():
+                backward_copy(high, d).wait_send()
+                backward_copy(low, d).wait_send()
 
         for d in range(4):
             @pl.when(inside(OFFSETS[d]))
             def _():
-                backward_copy(n, d).wait_recv()
-
-        more = dot(pick_t[...], back_in[n])
-        for c in range(comps):
-            a_ref[c] = base_ref[c] - dd_ref[n, c] * more[:, lanes(c)]
-        for d in range(4):
-            @pl.when(inside(-OFFSETS[d]))
-            def _():
-                backward_copy(n, d).wait_send()
-
-        @pl.when(level == half)
+                backward_copy(low, d).wait_recv()
+
+        last_ref[:ghosts, :] = back_in[low]
+        more = dot(pick_t2[...], last_ref[...])
+        for c in range(comps):
+            a_ref[c] = base_ref[c] - dd_ref[low, c] * more[:, lanes(c)]
+
+        @pl.when(low == half)
         def _():
             for c in range(comps):
                 hand_ref[c] = a_ref[c]
@@ -354,7 +508,7 @@
     def _():
         for c in range(comps):
             a_ref[c] = a_ref[c] + weight_ref[c] * u_ref[c]
-        lax.fori_loop(0, levels, backward, 0)
+        lax.fori_loop(0, levels // 2, backward, 0)
         hand_copy().start()
         rows_ref[sp] = row_ref[...]
 
@@ -392,6 +546,11 @@
         for level in range(half):
             factor_copy(level, 0).wait_send()
             factor_copy(level, 1).wait_send()
+        for level in range(1, half, 2):
+            for d in range(4):
+                @pl.when(inside(OFFSETS[d]))
+                def _():
+                    ghost_copy(level, d).wait_send()
 
 
 def shards(
@@ -445,7 +604,7 @@
             pltpu.VMEM((ghosts, blocks), BF16),
             pltpu.VMEM((blocks, ghosts), BF16),
             pltpu.VMEM((half, ghosts, wide), BF16),
-            pltpu.VMEM((half, ghosts, wide), BF16),
+            pltpu.VMEM((levels, ghosts, wide), BF16),
             pltpu.VMEM((levels, ghosts, wide), BF16),
             pltpu.VMEM((levels, ghosts, wide), BF16),
             pltpu.VMEM((slots, comps * blocks, nodes), F32),
@@ -457,6 +616,16 @@
             pltpu.VMEM((comps * ghosts, (slots - 1) * nodes), BF16),
             pltpu.VMEM((1, nodes), F32),
             pltpu.VMEM((n_space, 1, nodes), F32),
+            pltpu.VMEM((blocks, 2 * ghosts), BF16),
+            pltpu.VMEM((blocks, wide), BF16),
+            pltpu.VMEM(field, F32),
+            pltpu.VMEM(((slots - 1) * ghosts, 4 * ghosts), BF16),
+            pltpu.VMEM(((slots - 1) * ghosts, 4 * ghosts), BF16),
+            pltpu.VMEM((ghosts, nodes), BF16),
+            pltpu.VMEM((ghosts, nodes), BF16),
+            pltpu.VMEM((levels // 2, ghosts, wide), BF16),
+            pltpu.VMEM((levels // 2, 4, ghosts, wide), BF16),
+            pltpu.VMEM((2 * ghosts, wide), BF16),
             dma((8,)),
             dma((half, 4)),
             dma((half, 4)),
@@ -466,6 +635,11 @@
             dma((2, 2, half)),
             dma((n_dev,)),
             dma((n_space,)),
+            dma((2, 4)),
+            dma((2, 4)),
+            dma((2, half // 2, 4)),
+            dma((levels // 2, 16)),
+            dma((levels // 2, 16)),
         ],
         compiler_params=pltpu.CompilerParams(
             collective_id=0, has_side_effects=True, vmem_limit_bytes=60 * 1024 * 1024

time: 57.5 us -> 55.9 us (0.972)
  Pallas kernels: 54.3 us -> 52.8 us
    pallas_call x1, Pallas kernels: 54.3 us -> 52.8 us  [shards(): pl.pallas_call(functools.partial(window_kernel, dims), out_shape=(jax.Sha...]
where the time goes in v1:
time: 55.9 us; the launch traced here: 55.7 us
  Pallas kernels  52.8 us (94%)
  local copies, waits for them, and re-layouts  2.23 us (4%)
  between operations  0.65 us (1%)
    pallas_call x1, Pallas kernels, shards(): pl.pallas_call(functools.partial(window_kernel, dims), out_shape=(jax.Sha...  52.8 us
    unnamed x4, local copies, waits for them, and re-layouts  2.23 us

profile of v1, /device:TPU:1, one launch (start us, length us, event | category | flops | bytes accessed | tf_op | source)
XLA Modules:
  0.0 55.7 jit_solution(14305129024808004184)
XLA Ops:
  0.6 52.8 %window.1 = (f32[1,5,128,128]{3,2,1,0:T(8,128)}, f32[8]{0:T(128)}) custom-call(f32[8]{0:T(128)} %pitch_ref.1, f32[5,5,5]{2,1,0:T(8,128)} %mixing_ref.1, f32[1,5,128,128]{3,2,1,0:T(8,128)} %cp_hbm.1, f32[2,5,128,128]{3,2,1,0:T(8,128)} %src_hbm.1, f32[128,128]{1,0:T(8,128)} %metric_hbm.1, f32[5,128,128]{2,1,0:T(8,128)} %weight_hbm.1, f32[5,128,128]{2,1,0:T(8,128)} %end_hbm.1, ...), custom_call_target="tpu_custom_call" | custom-call | tf_op jit(solution)/shard_map/window/pallas_call | solution.py:577
  53.4 0.0 copy-start
  53.4 1.7 %copy.14 = f32[1,5,128,128]{3,2,1,0:T(8,128)} copy(f32[1,5,128,128]{3,2,1,0:T(8,128)} %get-tuple-element.4) | data formatting | bytes 655360
  55.1 0.0 copy-done
  55.1 0.5 copy.15
Async XLA Ops:
  53.4 1.7 %copy-start = (f32[8]{0:T(128)S(1)}, f32[8]{0:T(128)}, u32[]{:S(2)}) copy-start(f32[8]{0:T(128)} %get-tuple-element.5) | copy-start | bytes 100

commit v2 on v1

v2 whole, which is shorter than its diff:
```python
import functools
import math

import jax
import jax.numpy as jnp
from jax import lax
from jax.experimental import pallas as pl
from jax.experimental.pallas import tpu as pltpu
from jax.sharding import PartitionSpec as P

OFFSETS = (1, -1, 2, -2)
STEP_SIZE = 0.5
F32 = jnp.float32
BF16 = jnp.bfloat16
MESH = pl.DeviceIdType.MESH
DIRS = range(4)


def dot(a, b):
    return jnp.dot(a, b, preferred_element_type=F32)


def one_hot(hit):
    return hit.astype(F32).astype(BF16)


def beside(parts):
    return jnp.concatenate(list(parts), axis=1)


def below(parts):
    return jnp.concatenate(list(parts), axis=0)


def rounds_of(n_space):
    reach, rounds = 2 * max(OFFSETS), []
    while reach < n_space - 1:
        rounds.append(reach)
        reach *= 2
    return rounds


def window_kernel(
    dims,
    pitch_hbm, mixing_hbm, cp_hbm, src_hbm, metric_hbm, weight_hbm, end_hbm, lift_hbm, faces_hbm, send_hbm,
    out_ref, grad_ref,
    pitch_ref, mixing_ref, u_ref, lift_ref, faces_ref, send_ref, src_ref, metric_ref, weight_ref, a_ref, hand_ref,
    base_ref, dd_ref, wu_ref, lift_t, sq_ref,
    p_own, p_halo, pt_own, pt_halo, pick, pick_t, pick_t2, out_buf, in_buf, back_out, back_in, y_ref, yh_ref, z_ref,
    mixed_ref, g_ref, gw_ref, gh_ref, split_ref, wf_ref, row_ref, rows_ref,
    et_out, et_in, mg_out, mg_in, dup_out, dup_in, last_ref,
    load_sems, send_sems, recv_sems, bsend_sems, brecv_sems, hand_sems, factor_sems, gsend_sems, grecv_sems,
    table_sems, metric_sems, ghost_sems, dsend_sems, drecv_sems, round_sems,
):
    comps, blocks, nodes, slots, halo, half, n_tm, n_space, norm = dims
    ghosts = 4 * halo
    faces_n = slots - 1
    tm = lax.axis_index("tm")
    sp = lax.axis_index("space")
    n_dev = n_tm * n_space
    me = tm * n_space + sp
    lead = tm == n_tm - 1
    partner = (n_tm - 1 - tm, sp)
    levels = half * n_tm
    rounds = rounds_of(n_space)
    chunk = 32

    pairs = [
        (send_hbm, send_ref),
        (cp_hbm.at[0], u_ref),
        (faces_hbm, faces_ref),
        (pitch_hbm, pitch_ref),
        (mixing_hbm, mixing_ref),
        (lift_hbm, lift_ref),
        (metric_hbm, metric_ref),
        (weight_hbm, weight_ref),
        (src_hbm, src_ref),
        (end_hbm, a_ref),
    ]
    loads = [pltpu.make_async_copy(src, dst, load_sems.at[i]) for i, (src, dst) in enumerate(pairs)]
    for load in loads:
        load.start()

    in_buf[...] = jnp.zeros_like(in_buf)

    @pl.when(lead)
    def _():
        et_in[...] = jnp.zeros_like(et_in)
        mg_in[...] = jnp.zeros_like(mg_in)

    barrier = pltpu.get_barrier_semaphore()

    def inside(shift):
        return (sp + shift >= 0) & (sp + shift < n_space)

    def at(shift):
        return jnp.clip(sp + shift, 0, n_space - 1)

    met = n_tm - 1
    pl.semaphore_signal(barrier, inc=1, device_id=partner, device_id_type=MESH)
    for shift in OFFSETS:
        met = met + n_tm * inside(shift).astype(jnp.int32)

        @pl.when(inside(shift))
        def _():
            for side in range(n_tm):
                pl.semaphore_signal(barrier, inc=1, device_id=(side, at(shift)), device_id_type=MESH)

    def lanes(c):
        return slice(c * nodes, (c + 1) * nodes)

    def target(shift):
        return (tm, at(shift))

    def forward_copy(n, d):
        return pltpu.make_async_remote_copy(
            src_ref=out_buf.at[n, d], dst_ref=in_buf.at[tm * half + n, d],
            send_sem=send_sems.at[n, d], recv_sem=recv_sems.at[n, d],
            device_id=target(OFFSETS[d]), device_id_type=MESH,
        )

    def ghost_copy(n, d):
        return pltpu.make_async_remote_copy(
            src_ref=out_buf.at[n, d], dst_ref=in_buf.at[n, d],
            send_sem=ghost_sems.at[0, n // 2, d], recv_sem=ghost_sems.at[1, n // 2, d],
            device_id=(n_tm - 1, at(OFFSETS[d])), device_id_type=MESH,
        )

    def metric_copy(d):
        return pltpu.make_async_remote_copy(
            src_ref=mg_out.at[d], dst_ref=mg_in.at[d],
            send_sem=metric_sems.at[0, d], recv_sem=metric_sems.at[1, d],
            device_id=target(OFFSETS[d]), device_id_type=MESH,
        )

    def table_copy(d):
        rows = pl.ds(d * faces_n * halo, faces_n * halo)
        return pltpu.make_async_remote_copy(
            src_ref=et_out.at[rows], dst_ref=et_in.at[rows],
            send_sem=table_sems.at[0, d], recv_sem=table_sems.at[1, d],
            device_id=target(-OFFSETS[d]), device_id_type=MESH,
        )

    def second_copy(slot, d, far):
        return pltpu.make_async_remote_copy(
            src_ref=dup_out.at[slot, far], dst_ref=dup_in.at[slot, d, far],
            send_sem=dsend_sems.at[slot, 4 * d + far], recv_sem=drecv_sems.at[slot, 4 * d + far],
            device_id=target(-OFFSETS[far] - OFFSETS[d]), device_id_type=MESH,
        )

    second_pairs = [(d, far) for d in DIRS for far in DIRS if OFFSETS[d] + OFFSETS[far] != 0]
    second_pairs = sorted(second_pairs, key=lambda p: -abs(OFFSETS[p[0]] + OFFSETS[p[1]]))

    def backward_copy(n, d):
        return pltpu.make_async_remote_copy(
            src_ref=back_out.at[n, d], dst_ref=back_in.at[n, d],
            send_sem=bsend_sems.at[n, d], recv_sem=brecv_sems.at[n, d],
            device_id=target(-OFFSETS[d]), device_id_type=MESH,
        )

    def coef(k, e, c):
        return mixing_ref[k, e, c]

    def turn_of(level):
        angle = jnp.full((8, nodes), pitch_ref[level], F32)
        return jnp.cos(angle)[0:1], jnp.sin(angle)[0:1]

    def ghost_rows(ref, index, c):
        return below(ref[index + (d, c)] for d in DIRS)

    def ghost_wide(ref, index):
        return beside(ghost_rows(ref, index, c) for c in range(comps))

    def squash_and_pick(n):
        for c in range(comps):
            sq_ref[c] = jnp.tanh(u_ref[c]).astype(BF16)
        picked = dot(pick[...], beside(sq_ref[c] for c in range(comps))).astype(BF16)
        for d in DIRS:
            for c in range(comps):
                out_buf[n, d, c] = picked[d * halo : (d + 1) * halo, lanes(c)]

    row_ids = lax.broadcasted_iota(jnp.int32, (blocks, blocks), 0)
    lane_ids = lax.broadcasted_iota(jnp.int32, (blocks, blocks), 1)
    loads[0].wait()
    wanted = beside(
        [send_ref[0, d : d + 1, :] for d in DIRS] + [jnp.full((1, blocks - ghosts), -1, jnp.int32)]
    )
    spread = jnp.broadcast_to(wanted, (blocks, blocks))
    spread_t = jnp.transpose(spread.astype(F32)).astype(jnp.int32)
    pick[...] = one_hot(spread_t[:ghosts] == lane_ids[:ghosts])
    loads[1].wait()
    squash_and_pick(0)
    pl.semaphore_wait(barrier, met)
    for d in DIRS:
        @pl.when(inside(OFFSETS[d]))
        def _():
            forward_copy(0, d).start()

    pick_t[...] = one_hot(spread == row_ids)[:, :ghosts]
    doubled = beside([wanted[:, :ghosts]] * 2)
    pick_t2[...] = one_hot(jnp.broadcast_to(doubled, (blocks, 2 * ghosts)) == row_ids)
    row_ref[...] = jnp.zeros_like(row_ref)
    loads[2].wait()
    face_cols = []
    for k in range(faces_n):
        turned = jnp.broadcast_to(faces_ref[k : k + 1, :], (blocks, blocks))
        col = jnp.transpose(turned.astype(F32)).astype(jnp.int32)
        face_cols.append(col)
        p_own[k * blocks : (k + 1) * blocks, :] = one_hot(col == lane_ids)
        pt_own[k * blocks : (k + 1) * blocks, :] = one_hot(turned == row_ids)
        hit = one_hot(turned[:ghosts] == row_ids[:ghosts] + blocks)
        pt_halo[k * ghosts : (k + 1) * ghosts, :blocks] = hit
        pt_halo[k * ghosts : (k + 1) * ghosts, blocks:] = hit
    for pair in range(faces_n // 2):
        low = lane_ids < ghosts
        col = jnp.where(low, face_cols[2 * pair], face_cols[2 * pair + 1])
        want = jnp.where(low, lane_ids, lane_ids - ghosts) + blocks
        p_halo[:, pair * 2 * ghosts : (pair + 1) * 2 * ghosts] = one_hot(col == want)

    for load in loads[3:]:
        load.wait()
    for k in range(slots):
        lift_t[:, k * nodes : (k + 1) * nodes] = jnp.transpose(lift_ref[k].astype(F32)).astype(BF16)

    @pl.when(lead)
    def _():
        back_in[...] = jnp.zeros_like(back_in)
        dup_in[...] = jnp.zeros_like(dup_in)
        four = beside([wanted[:, :ghosts]] * 4)
        ids = lax.broadcasted_iota(jnp.int32, (blocks, 4 * ghosts), 0)
        picks = one_hot(jnp.broadcast_to(four, (blocks, 4 * ghosts)) == ids)
        table = dot(pt_halo[:, :blocks], picks)
        part = lax.broadcasted_iota(jnp.int32, (halo, 4 * ghosts), 1) // ghosts
        for d in DIRS:
            for k in range(faces_n):
                piece = table[k * ghosts + d * halo : k * ghosts + (d + 1) * halo]
                to = (d * faces_n + k) * halo
                et_out[to : to + halo, :] = jnp.where(part == d, piece, 0.0).astype(BF16)
        chosen = dot(pick[...], metric_ref[...].astype(BF16)).astype(BF16)
        for d in DIRS:
            mg_out[d] = chosen[d * halo : (d + 1) * halo]
        for d in DIRS:
            @pl.when(inside(OFFSETS[d]))
            def _():
                metric_copy(d).start()

            @pl.when(inside(-OFFSETS[d]))
            def _():
                table_copy(d).start()

    def factor_copy(level, which):
        ref = (dd_ref, wu_ref)[which]
        return pltpu.make_async_remote_copy(
            src_ref=ref.at[level], dst_ref=ref.at[level], send_sem=factor_sems.at[0, which, level],
            recv_sem=factor_sems.at[1, which, level], device_id=partner, device_id_type=MESH,
        )

    def round_signal(r):
        for side, shift in enumerate((rounds[r], -rounds[r])):
            @pl.when(inside(shift))
            def _():
                pl.semaphore_signal(
                    round_sems.at[r, side], inc=1, device_id=(n_tm - 1, at(shift)), device_id_type=MESH
                )

    def round_wait(r):
        for side, shift in enumerate((rounds[r], -rounds[r])):
            @pl.when(inside(-shift))
            def _():
                pl.semaphore_wait(round_sems.at[r, side], 1)

    def round_step(r):
        if 0 < r <= len(rounds):
            round_wait(r - 1)
        if r < len(rounds):
            round_signal(r)

    def forward(n, carry):
        level = tm * half + n
        active = (n < half - 1) | lead

        @pl.when(n > 0)
        def _():
            squash_and_pick(n)
            for d in DIRS:
                @pl.when(inside(OFFSETS[d]) & active)
                def _():
                    forward_copy(n, d).start()

                @pl.when(inside(OFFSETS[d]) & jnp.logical_not(lead) & (lax.rem(n, 2) == 1))
                def _():
                    ghost_copy(n, d).start()

        for r in range(half - 1):
            @pl.when(lead & (n == r + 1))
            def _():
                round_step(r)

        keep = jnp.where(level > 0, 1.0, 0.0).astype(F32)
        for c in range(comps):
            state = u_ref[c]
            t = jnp.tanh(state)
            dd_ref[level, c] = STEP_SIZE * (1.0 - t * t)
            wu_ref[level, c] = (keep * weight_ref[c]) * state

        @pl.when(jnp.logical_not(lead))
        def _():
            factor_copy(level, 0).start()
            factor_copy(level, 1).start()

        @pl.when(active)
        def _():
            cosine, sine = turn_of(level)
            squashed = beside(sq_ref[c] for c in range(comps))
            for k in range(slots):
                if k == 0:
                    stacked = sq_ref[...].reshape(comps * blocks, nodes)
                else:
                    got = dot(p_own[(k - 1) * blocks : k * blocks, :], squashed).astype(BF16)
                    stacked = below(got[:, lanes(c)] for c in range(comps))
                y_ref[k] = dot(stacked, lift_t[:, lanes(k)])

            def own_mix(r, carry):
                start = pl.multiple_of(r * chunk, chunk)
                metric_half = STEP_SIZE * metric_ref[pl.ds(start, chunk), :]
                sums = [None] * comps
                for k in range(slots):
                    for c in range(comps):
                        term = y_ref[k, pl.ds(c * blocks + start, chunk), :]
                        for e in range(comps):
                            add = coef(k, e, c) * term
                            sums[e] = add if sums[e] is None else sums[e] + add
                for e in range(comps):
                    rows = pl.ds(start, chunk)
                    forcing = cosine * src_ref[0, e, rows, :] + sine * src_ref[1, e, rows, :]
                    base_ref[e, rows, :] = u_ref[e, rows, :] + STEP_SIZE * forcing - metric_half * sums[e]
                return carry

            lax.fori_loop(0, blocks // chunk, own_mix, 0)

            for d in DIRS:
                @pl.when(inside(OFFSETS[d]))
                def _():
                    forward_copy(n, d).wait_send()

            for d in DIRS:
                @pl.when(inside(-OFFSETS[d]))
                def _():
                    forward_copy(n, d).wait_recv()

            stacked = below(ghost_rows(in_buf, (level,), c) for c in range(comps))
            yh_ref[...] = dot(stacked, lift_t[:, nodes:])
            for k in range(1, slots):
                for part in range(ghosts // chunk):
                    for e in range(comps):
                        total = None
                        for c in range(comps):
                            row = c * ghosts + part * chunk
                            add = coef(k, e, c) * yh_ref[row : row + chunk, lanes(k - 1)]
                            total = add if total is None else total + add
                        row = (k - 1) * ghosts + part * chunk
                        z_ref[e, row : row + chunk, :] = total.astype(BF16)
            more = dot(p_halo[...], beside(z_ref[e] for e in range(comps)))
            half_metric = STEP_SIZE * metric_ref[...]
            for e in range(comps):
                u_ref[e] = base_ref[e] - half_metric * more[:, lanes(e)]

        return carry

    lax.fori_loop(0, half, forward, 0)

    def hand_copy():
        return pltpu.make_async_remote_copy(
            src_ref=a_ref, dst_ref=out_ref.at[0], send_sem=hand_sems.at[0], recv_sem=hand_sems.at[1],
            device_id=partner, device_id_type=MESH,
        )

    def keep_copy():
        return pltpu.make_async_copy(hand_ref, out_ref.at[0], hand_sems.at[2])

    def grad_copy(source, other):
        return pltpu.make_async_remote_copy(
            src_ref=row_ref, dst_ref=rows_ref.at[source], send_sem=gsend_sems.at[other],
            recv_sem=grecv_sems.at[source], device_id=(other // n_space, lax.rem(other, n_space)),
            device_id_type=MESH,
        )

    def mix_back(k, row, rows, to):
        for c in range(comps):
            total = None
            for e in range(comps):
                add = coef(k, e, c) * gw_ref[row : row + rows, lanes(e)]
                total = add if total is None else total + add
            gh_ref[k - 1, c * ghosts + to : c * ghosts + to + rows, :] = total.astype(BF16)

    def lift_back():
        return dot(beside(gh_ref[k] for k in range(faces_n)), lift_ref[1:].reshape(faces_n * nodes, nodes))

    def halo_part(ref, level, keep):
        for e in range(comps):
            w = metric_ref[...] * ref[e]
            if keep:
                wf_ref[e] = w
            high = w.astype(BF16)
            split_ref[e, :blocks, :] = high
            split_ref[e, blocks:, :] = (w - high.astype(F32)).astype(BF16)
        gw_ref[...] = dot(pt_halo[...], beside(split_ref[e] for e in range(comps)))
        for k in range(1, slots):
            for part in range(ghosts // chunk):
                mix_back(k, (k - 1) * ghosts + part * chunk, chunk, part * chunk)
        lifted = lift_back().astype(BF16)
        for d in DIRS:
            for c in range(comps):
                row = c * ghosts + d * halo
                back_out[level, d, c] = lifted[row : row + halo]
        for d in DIRS:
            @pl.when(inside(-OFFSETS[d]))
            def _():
                backward_copy(level, d).start()

    def own_part(level):
        for k in range(slots):
            for r in range(blocks // chunk):
                rows = slice(r * chunk, (r + 1) * chunk)
                weighted = [wf_ref[e, rows, :] for e in range(comps)]
                for c in range(comps):
                    total = None
                    for e in range(comps):
                        add = coef(k, e, c) * weighted[e]
                        total = add if total is None else total + add
                    if k == 0:
                        g_ref[0, c * blocks + r * chunk : c * blocks + (r + 1) * chunk, :] = total.astype(BF16)
                    else:
                        mixed_ref[k - 1, c, rows, :] = total.astype(BF16)
            if k > 0:
                wide = beside(mixed_ref[k - 1, c] for c in range(comps))
                got = dot(pt_own[(k - 1) * blocks : k * blocks, :], wide).astype(BF16)
                for c in range(comps):
                    g_ref[k, c * blocks : (c + 1) * blocks, :] = got[:, lanes(c)]
        pushed = dot(beside(g_ref[k] for k in range(slots)), lift_ref[...].reshape(slots * nodes, nodes))
        for c in range(comps):
            base_ref[c] = a_ref[c] + wu_ref[level, c] - dd_ref[level, c] * pushed[c * blocks : (c + 1) * blocks]

    def add_grad(level):
        cosine, sine = turn_of(level)
        sums = None
        for e in range(comps):
            part = a_ref[e] * (cosine * src_ref[1, e] - sine * src_ref[0, e])
            sums = part if sums is None else sums + part
        value = jnp.sum(jnp.sum(sums, axis=0, keepdims=True), axis=1, keepdims=True) * (STEP_SIZE / norm)
        spots = lax.broadcasted_iota(jnp.int32, (1, nodes), 1)
        row_ref[...] = row_ref[...] + jnp.where(spots == level, value, 0.0)

    def backward(j, carry):
        high = levels - 1 - 2 * j
        low = high - 1

        halo_part(a_ref, high, True)

        @pl.when(j == 0)
        def _():
            for d in DIRS:
                @pl.when(inside(-OFFSETS[d]))
                def _():
                    metric_copy(d).wait_recv()

        @pl.when(high < half)
        def _():
            for d in DIRS:
                @pl.when(inside(-OFFSETS[d]))
                def _():
                    ghost_copy(high, d).wait_recv()

            for which in range(2):
                factor_copy(high, which).wait_recv()
                factor_copy(low, which).wait_recv()

        for far in DIRS:
            spread_metric = mg_in[far].astype(F32)
            d = OFFSETS.index(-OFFSETS[far])
            for c in range(comps):
                t = in_buf[high, far, c].astype(F32)
                factor = spread_metric * (STEP_SIZE - STEP_SIZE * t * t)
                scaled = (factor * back_out[high, far, c].astype(F32)).astype(BF16)
                dup_out[j, far, c] = scaled
                dup_in[j, d, far, c] = scaled
        for d, far in second_pairs:
            @pl.when(inside(-OFFSETS[far]) & inside(-OFFSETS[far] - OFFSETS[d]))
            def _():
                second_copy(j, d, far).start()

        own_part(high)
        halo_part(base_ref, low, False)
        add_grad(high)

        for d in DIRS:
            @pl.when(inside(OFFSETS[d]))
            def _():
                backward_copy(high, d).wait_recv()

        more = dot(pick_t[...], ghost_wide(back_in, (high,)))
        for c in range(comps):
            state = base_ref[c] - dd_ref[high, c] * more[:, lanes(c)]
            a_ref[c] = state
            wf_ref[c] = metric_ref[...] * state

        add_grad(low)

        @pl.when(low == 0)
        def _():
            def tell(r, carry):
                grad_copy(sp, lax.rem(me + r, n_dev)).start()
                return carry

            lax.fori_loop(1, n_dev, tell, 0)

        own_part(low)

        @pl.when(j == 0)
        def _():
            for d in DIRS:
                @pl.when(inside(OFFSETS[d]))
                def _():
                    table_copy(d).wait_recv()
                    metric_copy(d).wait_send()

                @pl.when(inside(-OFFSETS[d]))
                def _():
                    table_copy(d).wait_send()

        for d, far in second_pairs:
            @pl.when(inside(OFFSETS[d]) & inside(OFFSETS[d] + OFFSETS[far]))
            def _():
                second_copy(j, d, far).wait_recv()

        rows = [below(dup_in[j, d, far, c] for d in DIRS for far in DIRS) for c in range(comps)]
        gw_ref[...] = dot(et_in[...], beside(rows))
        for k in range(1, slots):
            for d in DIRS:
                mix_back(k, (d * faces_n + k - 1) * halo, halo, d * halo)
        lifted = (-lift_back()).astype(BF16)
        for c in range(comps):
            last_ref[c] = lifted[c * ghosts : (c + 1) * ghosts]

        for d, far in second_pairs:
            @pl.when(inside(-OFFSETS[far]) & inside(-OFFSETS[far] - OFFSETS[d]))
            def _():
                second_copy(j, d, far).wait_send()
        for d in DIRS:
            @pl.when(inside(-OFFSETS[d]))
            def _():
                backward_copy(high, d).wait_send()
                backward_copy(low, d).wait_send()

        for d in DIRS:
            @pl.when(inside(OFFSETS[d]))
            def _():
                backward_copy(low, d).wait_recv()

        late = beside(below([ghost_rows(back_in, (low,), c), last_ref[c]]) for c in range(comps))
        more = dot(pick_t2[...], late)
        for c in range(comps):
            a_ref[c] = base_ref[c] - dd_ref[low, c] * more[:, lanes(c)]

        @pl.when(low == half)
        def _():
            for c in range(comps):
                hand_ref[c] = a_ref[c]
            keep_copy().start()

        return carry

    @pl.when(lead)
    def _():
        for r in range(half - 1, len(rounds) + 1):
            round_step(r)
        for c in range(comps):
            a_ref[c] = a_ref[c] + weight_ref[c] * u_ref[c]
        lax.fori_loop(0, levels // 2, backward, 0)
        hand_copy().start()
        rows_ref[sp] = row_ref[...]

        def settle(r, carry):
            other = lax.rem(sp + r, n_space)
            grad_copy(other, me).wait_recv()
            return carry

        lax.fori_loop(1, n_space, settle, 0)

    @pl.when(jnp.logical_not(lead))
    def _():
        def settle(r, carry):
            grad_copy(r, me).wait_recv()
            return carry

        lax.fori_loop(0, n_space, settle, 0)

    grad_ref[...] = jnp.sum(rows_ref[...], axis=0)[0, : grad_ref.shape[0]]

    @pl.when(lead)
    def _():
        hand_copy().wait_send()
        keep_copy().wait()

        def sent(r, carry):
            grad_copy(sp, lax.rem(me + r, n_dev)).wait_send()
            return carry

        lax.fori_loop(1, n_dev, sent, 0)

    @pl.when(jnp.logical_not(lead))
    def _():
        hand_copy().wait_recv()
        for level in range(half):
            factor_copy(level, 0).wait_send()
            factor_copy(level, 1).wait_send()
        for level in range(1, half, 2):
            for d in DIRS:
                @pl.when(inside(OFFSETS[d]))
                def _():
                    ghost_copy(level, d).wait_send()


def shards(
    checkpoints, sources, pitch, metric, obj_weight, adjoint_end, lift, mixing, faces, send_idx
):
    comps = sources.shape[1]
    blocks, nodes = metric.shape
    slots = lift.shape[0]
    faces_n = slots - 1
    halo = send_idx.shape[2]
    n_tm = lax.axis_size("tm")
    n_space = lax.axis_size("space")
    levels = pitch.shape[0]
    half = levels // n_tm
    twos = levels // 2
    ghosts = 4 * halo
    norm = math.sqrt(comps * nodes * blocks * n_space)
    wide = comps * nodes
    field = (comps, blocks, nodes)
    group = (4, comps, halo, nodes)
    vmem = pl.BlockSpec(memory_space=pltpu.VMEM)
    anym = pl.BlockSpec(memory_space=pl.ANY)
    dma = pltpu.SemaphoreType.DMA
    n_dev = n_tm * n_space
    dims = (comps, blocks, nodes, slots, halo, half, n_tm, n_space, norm)
    bounds, grad = pl.pallas_call(
        functools.partial(window_kernel, dims),
        out_shape=(
            jax.ShapeDtypeStruct((1, *field), F32),
            jax.ShapeDtypeStruct((levels,), F32),
        ),
        in_specs=[anym] * 10,
        out_specs=(anym, vmem),
        scratch_shapes=[
            pltpu.SMEM(pitch.shape, F32),
            pltpu.SMEM(mixing.shape, F32),
            pltpu.VMEM(field, F32),
            pltpu.VMEM(lift.shape, BF16),
            pltpu.VMEM(faces.shape[::-1], jnp.int32),
            pltpu.VMEM(send_idx.shape, jnp.int32),
            pltpu.VMEM((2, *field), F32),
            pltpu.VMEM((blocks, nodes), F32),
            pltpu.VMEM(field, F32),
            pltpu.VMEM(field, F32),
            pltpu.VMEM(field, F32),
            pltpu.VMEM(field, F32),
            pltpu.VMEM((levels, *field), F32),
            pltpu.VMEM((levels, *field), F32),
            pltpu.VMEM((nodes, slots * nodes), BF16),
            pltpu.VMEM(field, BF16),
            pltpu.VMEM((faces_n * blocks, blocks), BF16),
            pltpu.VMEM((blocks, faces_n * ghosts), BF16),
            pltpu.VMEM((faces_n * blocks, blocks), BF16),
            pltpu.VMEM((faces_n * ghosts, 2 * blocks), BF16),
            pltpu.VMEM((ghosts, blocks), BF16),
            pltpu.VMEM((blocks, ghosts), BF16),
            pltpu.VMEM((blocks, 2 * ghosts), BF16),
            pltpu.VMEM((half, *group), BF16),
            pltpu.VMEM((levels, *group), BF16),
            pltpu.VMEM((levels, *group), BF16),
            pltpu.VMEM((levels, *group), BF16),
            pltpu.VMEM((slots, comps * blocks, nodes), F32),
            pltpu.VMEM((comps * ghosts, faces_n * nodes), F32),
            pltpu.VMEM((comps, faces_n * ghosts, nodes), BF16),
            pltpu.VMEM((faces_n, *field), BF16),
            pltpu.VMEM((slots, comps * blocks, nodes), BF16),
            pltpu.VMEM((faces_n * ghosts, wide), F32),
            pltpu.VMEM((faces_n, comps * ghosts, nodes), BF16),
            pltpu.VMEM((comps, 2 * blocks, nodes), BF16),
            pltpu.VMEM(field, F32),
            pltpu.VMEM((1, nodes), F32),
            pltpu.VMEM((n_space, 1, nodes), F32),
            pltpu.VMEM((faces_n * ghosts, 4 * ghosts), BF16),
            pltpu.VMEM((faces_n * ghosts, 4 * ghosts), BF16),
            pltpu.VMEM((4, halo, nodes), BF16),
            pltpu.VMEM((4, halo, nodes), BF16),
            pltpu.VMEM((twos, *group), BF16),
            pltpu.VMEM((twos, 4, *group), BF16),
            pltpu.VMEM((comps, ghosts, nodes), BF16),
            dma((10,)),
            dma((half, 4)),
            dma((half, 4)),
            dma((levels, 4)),
            dma((levels, 4)),
            dma((3,)),
            dma((2, 2, half)),
            dma((n_dev,)),
            dma((n_space,)),
            dma((2, 4)),
            dma((2, 4)),
            dma((2, half // 2, 4)),
            dma((twos, 16)),
            dma((twos, 16)),
            pltpu.SemaphoreType.REGULAR((max(1, len(rounds_of(n_space))), 2)),
        ],
        compiler_params=pltpu.CompilerParams(
            collective_id=0, has_side_effects=True, vmem_limit_bytes=60 * 1024 * 1024
        ),
        name="window",
    )(pitch, mixing, checkpoints, sources, metric, obj_weight, adjoint_end, lift, faces.T, send_idx)
    return bounds, grad


def solution(mesh):
    placed = (
        P("tm", None, "space", None),
        P(None, None, "space", None),
        P(),
        P("space", None),
        P(None, "space", None),
        P(None, "space", None),
        P(),
        P(),
        P("space", None),
        P("space", None, None),
    )
    return jax.shard_map(
        shards,
        mesh=mesh,
        in_specs=placed,
        out_specs=(P("tm", None, "space", None), P()),
        check_vma=False,
    )
```

time: 55.9 us -> 52.8 us (0.945)
  Pallas kernels: 52.8 us -> 49.7 us
    pallas_call x1, Pallas kernels: 52.8 us -> 49.7 us  [shards(): pl.pallas_call(functools.partial(window_kernel, dims), out_shape=(jax.Sha...]
where the time goes in v2:
time: 52.8 us; the launch traced here: 52.6 us
  Pallas kernels  49.7 us (94%)
  local copies, waits for them, and re-layouts  2.23 us (4%)
  between operations  0.65 us (1%)
    pallas_call x1, Pallas kernels, shards(): pl.pallas_call(functools.partial(window_kernel, dims), out_shape=(jax.Sha...  49.7 us
    unnamed x4, local copies, waits for them, and re-layouts  2.23 us

profile of v2, /device:TPU:1, one launch (start us, length us, event | category | flops | bytes accessed | tf_op | source)
XLA Modules:
  0.0 52.6 jit_solution(17630202798356689655)
XLA Ops:
  0.6 49.7 %window.1 = (f32[1,5,128,128]{3,2,1,0:T(8,128)}, f32[8]{0:T(128)}) custom-call(f32[8]{0:T(128)} %pitch_hbm.1, f32[5,5,5]{2,1,0:T(8,128)} %mixing_hbm.1, f32[1,5,128,128]{3,2,1,0:T(8,128)} %cp_hbm.1, f32[2,5,128,128]{3,2,1,0:T(8,128)} %src_hbm.1, f32[128,128]{1,0:T(8,128)} %metric_hbm.1, f32[5,128,128]{2,1,0:T(8,128)} %weight_hbm.1, f32[5,128,128]{2,1,0:T(8,128)} %end_hbm.1, ...), custom_call_target="tpu_custom_call" | custom-call | tf_op jit(solution)/shard_map/window/pallas_call | solution.py:647
  50.4 0.0 copy-start
  50.4 1.7 %copy.14 = f32[1,5,128,128]{3,2,1,0:T(8,128)} copy(f32[1,5,128,128]{3,2,1,0:T(8,128)} %get-tuple-element.4) | data formatting | bytes 655360
  52.1 0.0 copy-done
  52.1 0.5 copy.15
Async XLA Ops:
  50.4 1.7 %copy-start = (f32[8]{0:T(128)S(1)}, f32[8]{0:T(128)}, u32[]{:S(2)}) copy-start(f32[8]{0:T(128)} %get-tuple-element.5) | copy-start | bytes 100

commit v3 on v2

--- a/solution.py
+++ b/solution.py
@@ -48,9 +48,9 @@
     base_ref, dd_ref, wu_ref, lift_t, sq_ref,
     p_own, p_halo, pt_own, pt_halo, pick, pick_t, pick_t2, out_buf, in_buf, back_out, back_in, y_ref, yh_ref, z_ref,
     mixed_ref, g_ref, gw_ref, gh_ref, split_ref, wf_ref, row_ref, rows_ref,
-    et_out, et_in, mg_out, mg_in, dup_out, dup_in, last_ref,
+    et_out, et_in, mg_out, mg_in, dup_out, dup_in, last_ref, turn_ref, part_ref, hint_out, hint_in,
     load_sems, send_sems, recv_sems, bsend_sems, brecv_sems, hand_sems, factor_sems, gsend_sems, grecv_sems,
-    table_sems, metric_sems, ghost_sems, dsend_sems, drecv_sems, round_sems,
+    table_sems, metric_sems, ghost_sems, dsend_sems, drecv_sems, round_sems, hint_sems, keep_sems,
 ):
     comps, blocks, nodes, slots, halo, half, n_tm, n_space, norm = dims
     ghosts = 4 * halo
@@ -87,6 +87,7 @@
     def _():
         et_in[...] = jnp.zeros_like(et_in)
         mg_in[...] = jnp.zeros_like(mg_in)
+        hint_in[...] = jnp.zeros_like(hint_in)
 
     barrier = pltpu.get_barrier_semaphore()
 
@@ -123,6 +124,13 @@
         return pltpu.make_async_remote_copy(
             src_ref=out_buf.at[n, d], dst_ref=in_buf.at[n, d],
             send_sem=ghost_sems.at[0, n // 2, d], recv_sem=ghost_sems.at[1, n // 2, d],
+            device_id=(n_tm - 1, at(OFFSETS[d])), device_id_type=MESH,
+        )
+
+    def hint_copy(d):
+        return pltpu.make_async_remote_copy(
+            src_ref=hint_out.at[d], dst_ref=hint_in.at[d],
+            send_sem=hint_sems.at[0, d], recv_sem=hint_sems.at[1, d],
             device_id=(n_tm - 1, at(OFFSETS[d])), device_id_type=MESH,
         )
 
@@ -199,7 +207,7 @@
     pick_t[...] = one_hot(spread == row_ids)[:, :ghosts]
     doubled = beside([wanted[:, :ghosts]] * 2)
     pick_t2[...] = one_hot(jnp.broadcast_to(doubled, (blocks, 2 * ghosts)) == row_ids)
-    row_ref[...] = jnp.zeros_like(row_ref)
+    part_ref[...] = jnp.zeros_like(part_ref)
     loads[2].wait()
     face_cols = []
     for k in range(faces_n):
@@ -224,6 +232,12 @@
 
     @pl.when(lead)
     def _():
+        which = lax.broadcasted_iota(jnp.int32, (levels, nodes), 0)
+        angles = jnp.zeros((levels, nodes), F32)
+        for n in range(levels):
+            angles = jnp.where(which == n, pitch_ref[n], angles)
+        turn_ref[0] = jnp.cos(angles)
+        turn_ref[1] = jnp.sin(angles)
         back_in[...] = jnp.zeros_like(back_in)
         dup_in[...] = jnp.zeros_like(dup_in)
         four = beside([wanted[:, :ghosts]] * 4)
@@ -307,6 +321,22 @@
         def _():
             factor_copy(level, 0).start()
             factor_copy(level, 1).start()
+
+        @pl.when(level == 1)
+        def _():
+            cosine, sine = turn_of(0)
+            fields = []
+            for c in range(comps):
+                turning = cosine * src_ref[1, c] - sine * src_ref[0, c]
+                fields.append((dd_ref[1, c] * turning).astype(BF16))
+            chosen = dot(pick[...], beside(fields)).astype(BF16)
+            for d in DIRS:
+                for c in range(comps):
+                    hint_out[d, c] = chosen[d * halo : (d + 1) * halo, lanes(c)]
+            for d in DIRS:
+                @pl.when(inside(OFFSETS[d]))
+                def _():
+                    hint_copy(d).start()
 
         @pl.when(active)
         def _():
@@ -369,14 +399,14 @@
 
     lax.fori_loop(0, half, forward, 0)
 
-    def hand_copy():
-        return pltpu.make_async_remote_copy(
-            src_ref=a_ref, dst_ref=out_ref.at[0], send_sem=hand_sems.at[0], recv_sem=hand_sems.at[1],
+    def hand_copy(c):
+        return pltpu.make_async_remote_copy(
+            src_ref=a_ref.at[c], dst_ref=out_ref.at[0, c], send_sem=hand_sems.at[0, c], recv_sem=hand_sems.at[1, c],
             device_id=partner, device_id_type=MESH,
         )
 
     def keep_copy():
-        return pltpu.make_async_copy(hand_ref, out_ref.at[0], hand_sems.at[2])
+        return pltpu.make_async_copy(hand_ref, out_ref.at[0], keep_sems)
 
     def grad_copy(source, other):
         return pltpu.make_async_remote_copy(
@@ -418,8 +448,8 @@
             def _():
                 backward_copy(level, d).start()
 
-    def own_part(level):
-        for k in range(slots):
+    def own_mixing():
+        for k in [*range(1, slots), 0]:
             for r in range(blocks // chunk):
                 rows = slice(r * chunk, (r + 1) * chunk)
                 weighted = [wf_ref[e, rows, :] for e in range(comps)]
@@ -437,19 +467,25 @@
                 got = dot(pt_own[(k - 1) * blocks : k * blocks, :], wide).astype(BF16)
                 for c in range(comps):
                     g_ref[k, c * blocks : (c + 1) * blocks, :] = got[:, lanes(c)]
+
+    def own_lift(level):
         pushed = dot(beside(g_ref[k] for k in range(slots)), lift_ref[...].reshape(slots * nodes, nodes))
         for c in range(comps):
             base_ref[c] = a_ref[c] + wu_ref[level, c] - dd_ref[level, c] * pushed[c * blocks : (c + 1) * blocks]
 
-    def add_grad(level):
-        cosine, sine = turn_of(level)
-        sums = None
+    def add_grad(level, ref=a_ref, extra=None):
+        cosine, sine = turn_ref[0, pl.ds(level, 1), :], turn_ref[1, pl.ds(level, 1), :]
+        sums = extra
         for e in range(comps):
-            part = a_ref[e] * (cosine * src_ref[1, e] - sine * src_ref[0, e])
+            part = ref[e] * (cosine * src_ref[1, e] - sine * src_ref[0, e])
             sums = part if sums is None else sums + part
-        value = jnp.sum(jnp.sum(sums, axis=0, keepdims=True), axis=1, keepdims=True) * (STEP_SIZE / norm)
-        spots = lax.broadcasted_iota(jnp.int32, (1, nodes), 1)
-        row_ref[...] = row_ref[...] + jnp.where(spots == level, value, 0.0)
+        part_ref[pl.ds(level, 1), :] = jnp.sum(sums, axis=0, keepdims=True)
+
+    def total_grad():
+        values = jnp.sum(part_ref[...], axis=1, keepdims=True) * (STEP_SIZE / norm)
+        spots = lax.broadcasted_iota(jnp.int32, (levels, nodes), 1)
+        own = lax.broadcasted_iota(jnp.int32, (levels, nodes), 0)
+        row_ref[...] = jnp.sum(jnp.where(spots == own, values, 0.0), axis=0, keepdims=True)
 
     def backward(j, carry):
         high = levels - 1 - 2 * j
@@ -489,9 +525,32 @@
             def _():
                 second_copy(j, d, far).start()
 
-        own_part(high)
+        add_grad(high)
+        own_mixing()
+        own_lift(high)
         halo_part(base_ref, low, False)
-        add_grad(high)
+
+        @pl.when(low == 0)
+        def _():
+            for d in DIRS:
+                @pl.when(inside(-OFFSETS[d]))
+                def _():
+                    hint_copy(d).wait_recv()
+
+            missing = None
+            for d in DIRS:
+                for c in range(comps):
+                    part = back_out[high, d, c].astype(F32) * hint_in[d, c].astype(F32)
+                    missing = part if missing is None else missing + part
+            add_grad(low, base_ref, below([-missing, jnp.zeros((blocks - halo, nodes), F32)]))
+            total_grad()
+
+            def tell(r, carry):
+                other = lax.rem(me + r, n_dev)
+                grad_copy(sp, other).start()
+                return carry
+
+            lax.fori_loop(1, n_dev, tell, 0)
 
         for d in DIRS:
             @pl.when(inside(OFFSETS[d]))
@@ -506,15 +565,8 @@
 
         add_grad(low)
 
-        @pl.when(low == 0)
-        def _():
-            def tell(r, carry):
-                grad_copy(sp, lax.rem(me + r, n_dev)).start()
-                return carry
-
-            lax.fori_loop(1, n_dev, tell, 0)
-
-        own_part(low)
+        own_mixing()
+        own_lift(low)
 
         @pl.when(j == 0)
         def _():
@@ -522,11 +574,6 @@
                 @pl.when(inside(OFFSETS[d]))
                 def _():
                     table_copy(d).wait_recv()
-                    metric_copy(d).wait_send()
-
-                @pl.when(inside(-OFFSETS[d]))
-                def _():
-                    table_copy(d).wait_send()
 
         for d, far in second_pairs:
             @pl.when(inside(OFFSETS[d]) & inside(OFFSETS[d] + OFFSETS[far]))
@@ -541,16 +588,6 @@
         lifted = (-lift_back()).astype(BF16)
         for c in range(comps):
             last_ref[c] = lifted[c * ghosts : (c + 1) * ghosts]
-
-        for d, far in second_pairs:
-            @pl.when(inside(-OFFSETS[far]) & inside(-OFFSETS[far] - OFFSETS[d]))
-            def _():
-                second_copy(j, d, far).wait_send()
-        for d in DIRS:
-            @pl.when(inside(-OFFSETS[d]))
-            def _():
-                backward_copy(high, d).wait_send()
-                backward_copy(low, d).wait_send()
 
         for d in DIRS:
             @pl.when(inside(OFFSETS[d]))
@@ -577,8 +614,31 @@
         for c in range(comps):
             a_ref[c] = a_ref[c] + weight_ref[c] * u_ref[c]
         lax.fori_loop(0, levels // 2, backward, 0)
-        hand_copy().start()
+        for c in range(comps):
+            hand_copy(c).start()
         rows_ref[sp] = row_ref[...]
+
+        def drained(j, carry):
+            for d, far in second_pairs:
+                @pl.when(inside(-OFFSETS[far]) & inside(-OFFSETS[far] - OFFSETS[d]))
+                def _():
+                    second_copy(j, d, far).wait_send()
+            for d in DIRS:
+                @pl.when(inside(-OFFSETS[d]))
+                def _():
+                    backward_copy(2 * j, d).wait_send()
+                    backward_copy(2 * j + 1, d).wait_send()
+            return carry
+
+        lax.fori_loop(0, levels // 2, drained, 0)
+        for d in DIRS:
+            @pl.when(inside(OFFSETS[d]))
+            def _():
+                metric_copy(d).wait_send()
+
+            @pl.when(inside(-OFFSETS[d]))
+            def _():
+                table_copy(d).wait_send()
 
         def settle(r, carry):
             other = lax.rem(sp + r, n_space)
@@ -599,7 +659,8 @@
 
     @pl.when(lead)
     def _():
-        hand_copy().wait_send()
+        for c in range(comps):
+            hand_copy(c).wait_send()
         keep_copy().wait()
 
         def sent(r, carry):
@@ -610,15 +671,31 @@
 
     @pl.when(jnp.logical_not(lead))
     def _():
-        hand_copy().wait_recv()
+        for c in range(comps):
+            hand_copy(c).wait_recv()
         for level in range(half):
             factor_copy(level, 0).wait_send()
             factor_copy(level, 1).wait_send()
-        for level in range(1, half, 2):
-            for d in DIRS:
-                @pl.when(inside(OFFSETS[d]))
-                def _():
+        for d in DIRS:
+            @pl.when(inside(OFFSETS[d]))
+            def _():
+                hint_copy(d).wait_send()
+                for level in range(1, half, 2):
                     ghost_copy(level, d).wait_send()
+
+
+def finish_kernel(pieces, held_hbm, grad_hbm, out_hbm, grad_out, buf, row, sems):
+    inward = [pltpu.make_async_copy(held_hbm.at[0, c], buf.at[c], sems.at[0, c]) for c in range(pieces)]
+    outward = [pltpu.make_async_copy(buf.at[c], out_hbm.at[0, c], sems.at[1, c]) for c in range(pieces)]
+    inward.append(pltpu.make_async_copy(grad_hbm, row, sems.at[0, pieces]))
+    outward.append(pltpu.make_async_copy(row, grad_out, sems.at[1, pieces]))
+    for copy in inward:
+        copy.start()
+    for first, second in zip(inward, outward):
+        first.wait()
+        second.start()
+    for copy in outward:
+        copy.wait()
 
 
 def shards(
@@ -698,12 +775,16 @@
             pltpu.VMEM((twos, *group), BF16),
             pltpu.VMEM((twos, 4, *group), BF16),
             pltpu.VMEM((comps, ghosts, nodes), BF16),
+            pltpu.VMEM((2, levels, nodes), F32),
+            pltpu.VMEM((levels, nodes), F32),
+            pltpu.VMEM(group, BF16),
+            pltpu.VMEM(group, BF16),
             dma((10,)),
             dma((half, 4)),
             dma((half, 4)),
             dma((levels, 4)),
             dma((levels, 4)),
-            dma((3,)),
+            dma((2, comps)),
             dma((2, 2, half)),
             dma((n_dev,)),
             dma((n_space,)),
@@ -713,13 +794,26 @@
             dma((twos, 16)),
             dma((twos, 16)),
             pltpu.SemaphoreType.REGULAR((max(1, len(rounds_of(n_space))), 2)),
+            dma((2, 4)),
+            dma(()),
         ],
         compiler_params=pltpu.CompilerParams(
             collective_id=0, has_side_effects=True, vmem_limit_bytes=60 * 1024 * 1024
         ),
         name="window",
     )(pitch, mixing, checkpoints, sources, metric, obj_weight, adjoint_end, lift, faces.T, send_idx)
-    return bounds, grad
+    return pl.pallas_call(
+        functools.partial(finish_kernel, comps),
+        out_shape=(
+            jax.ShapeDtypeStruct((1, *field), F32),
+            jax.ShapeDtypeStruct((levels,), F32),
+        ),
+        in_specs=[anym] * 2,
+        out_specs=(anym, anym),
+        scratch_shapes=[pltpu.VMEM(field, F32), pltpu.VMEM((levels,), F32), dma((2, comps + 1))],
+        compiler_params=pltpu.CompilerParams(vmem_limit_bytes=60 * 1024 * 1024),
+        name="finish",
+    )(bounds, grad)
 
 
 def solution(mesh):

time: 52.8 us -> 51.5 us (0.975)
  local copies, waits for them, and re-layouts: 2.23 us -> 0 us
  Pallas kernels: 49.7 us -> 50.7 us
    unnamed x4 -> x0, local copies, waits for them, and re-layouts: 2.23 us -> none
    pallas_call x0 -> x1, Pallas kernels: none -> 1.7 us  [shards(): pl.pallas_call(functools.partial(finish_kernel, comps), out_shape=(jax.Sh...]
    pallas_call x1, Pallas kernels: 49.7 us -> 49 us  [shards(): pl.pallas_call(functools.partial(window_kernel, dims), out_shape=(jax.Sha...]
where the time goes in v3:
time: 51.5 us; the launch traced here: 51.3 us
  Pallas kernels  50.7 us (98%)
  between operations  0.64 us (1%)
    pallas_call x1, Pallas kernels, shards(): pl.pallas_call(functools.partial(window_kernel, dims), out_shape=(jax.Sha...  49 us
    pallas_call x1, Pallas kernels, shards(): pl.pallas_call(functools.partial(finish_kernel, comps), out_shape=(jax.Sh...  1.7 us

profile of v3, /device:TPU:1, one launch (start us, length us, event | category | flops | bytes accessed | tf_op | source)
XLA Modules:
  0.0 51.3 jit_solution(4705722340296338600)
XLA Ops:
  0.6 49.0 %window.1 = (f32[1,5,128,128]{3,2,1,0:T(8,128)}, f32[8]{0:T(128)}) custom-call(f32[8]{0:T(128)} %pitch_hbm.1, f32[5,5,5]{2,1,0:T(8,128)} %mixing_hbm.1, f32[1,5,128,128]{3,2,1,0:T(8,128)} %cp_hbm.1, f32[2,5,128,128]{3,2,1,0:T(8,128)} %src_hbm.1, f32[128,128]{1,0:T(8,128)} %metric_hbm.1, f32[5,128,128]{2,1,0:T(8,128)} %weight_hbm.1, f32[5,128,128]{2,1,0:T(8,128)} %end_hbm.1, ...), custom_call_target="tpu_custom_call" | custom-call | tf_op jit(solution)/shard_map/window/pallas_call | solution.py:724
  49.6 1.7 %finish.1 = (f32[1,5,128,128]{3,2,1,0:T(8,128)}, f32[8]{0:T(128)}) custom-call(f32[1,5,128,128]{3,2,1,0:T(8,128)} %get-tuple-element.4.held_hbm, f32[8]{0:T(128)} %get-tuple-element.5.grad_hbm), custom_call_target="tpu_custom_call" | custom-call | tf_op jit(solution)/shard_map/finish/pallas_call | solution.py:805

commit v4 on v3

--- a/solution.py
+++ b/solution.py
@@ -48,7 +48,7 @@
     base_ref, dd_ref, wu_ref, lift_t, sq_ref,
     p_own, p_halo, pt_own, pt_halo, pick, pick_t, pick_t2, out_buf, in_buf, back_out, back_in, y_ref, yh_ref, z_ref,
     mixed_ref, g_ref, gw_ref, gh_ref, split_ref, wf_ref, row_ref, rows_ref,
-    et_out, et_in, mg_out, mg_in, dup_out, dup_in, last_ref, turn_ref, part_ref, hint_out, hint_in,
+    et_out, et_in, mg_out, mg_in, dup_out, dup_in, last_ref, turn_ref, part_ref, hint_out, hint_in, near_ref, spot_metric, spot_base,
     load_sems, send_sems, recv_sems, bsend_sems, brecv_sems, hand_sems, factor_sems, gsend_sems, grecv_sems,
     table_sems, metric_sems, ghost_sems, dsend_sems, drecv_sems, round_sems, hint_sems, keep_sems,
 ):
@@ -227,6 +227,13 @@
 
     for load in loads[3:]:
         load.wait()
+    def picked_rows(value):
+        high = value.astype(BF16)
+        low = (value - high.astype(F32)).astype(BF16)
+        return dot(beside([pick[...], pick[...]]), below([high, low]))
+
+    near_ref[...] = dot(pick[...], p_halo[...]).astype(BF16)
+    spot_metric[...] = picked_rows(STEP_SIZE * metric_ref[...])
     for k in range(slots):
         lift_t[:, k * nodes : (k + 1) * nodes] = jnp.transpose(lift_ref[k].astype(F32)).astype(BF16)
 
@@ -295,15 +302,8 @@
 
         @pl.when(n > 0)
         def _():
-            squash_and_pick(n)
-            for d in DIRS:
-                @pl.when(inside(OFFSETS[d]) & active)
-                def _():
-                    forward_copy(n, d).start()
-
-                @pl.when(inside(OFFSETS[d]) & jnp.logical_not(lead) & (lax.rem(n, 2) == 1))
-                def _():
-                    ghost_copy(n, d).start()
+            for c in range(comps):
+                sq_ref[c] = jnp.tanh(u_ref[c]).astype(BF16)
 
         for r in range(half - 1):
             @pl.when(lead & (n == r + 1))
@@ -367,6 +367,7 @@
                 return carry
 
             lax.fori_loop(0, blocks // chunk, own_mix, 0)
+            spot_base[...] = picked_rows(beside(base_ref[e] for e in range(comps)))
 
             for d in DIRS:
                 @pl.when(inside(OFFSETS[d]))
@@ -390,6 +391,25 @@
                             total = add if total is None else total + add
                         row = (k - 1) * ghosts + part * chunk
                         z_ref[e, row : row + chunk, :] = total.astype(BF16)
+            later = n + 1
+
+            @pl.when(later < half)
+            def _():
+                more = dot(near_ref[...], beside(z_ref[e] for e in range(comps)))
+                for c in range(comps):
+                    spot = spot_base[:, lanes(c)] - spot_metric[...] * more[:, lanes(c)]
+                    value = jnp.tanh(spot).astype(BF16)
+                    for d in DIRS:
+                        out_buf[later, d, c] = value[d * halo : (d + 1) * halo]
+                for d in DIRS:
+                    @pl.when(inside(OFFSETS[d]) & ((later < half - 1) | lead))
+                    def _():
+                        forward_copy(later, d).start()
+
+                    @pl.when(inside(OFFSETS[d]) & jnp.logical_not(lead) & (lax.rem(later, 2) == 1))
+                    def _():
+                        ghost_copy(later, d).start()
+
             more = dot(p_halo[...], beside(z_ref[e] for e in range(comps)))
             half_metric = STEP_SIZE * metric_ref[...]
             for e in range(comps):
@@ -779,6 +799,9 @@
             pltpu.VMEM((levels, nodes), F32),
             pltpu.VMEM(group, BF16),
             pltpu.VMEM(group, BF16),
+            pltpu.VMEM((ghosts, faces_n * ghosts), BF16),
+            pltpu.VMEM((ghosts, nodes), F32),
+            pltpu.VMEM((ghosts, wide), F32),
             dma((10,)),
             dma((half, 4)),
             dma((half, 4)),

time: 51.5 us -> 50.7 us (0.984)
  Pallas kernels: 50.7 us -> 49.8 us
    pallas_call x1, Pallas kernels: 49 us -> 48.1 us  [shards(): pl.pallas_call(functools.partial(window_kernel, dims), out_shape=(jax.Sha...]
where the time goes in v4:
time: 50.7 us; the launch traced here: 50.5 us
  Pallas kernels  49.8 us (98%)
  between operations  0.64 us (1%)
    pallas_call x1, Pallas kernels, shards(): pl.pallas_call(functools.partial(window_kernel, dims), out_shape=(jax.Sha...  48.1 us
    pallas_call x1, Pallas kernels, shards(): pl.pallas_call(functools.partial(finish_kernel, comps), out_shape=(jax.Sh...  1.7 us

profile of v4, /device:TPU:1, one launch (start us, length us, event | category | flops | bytes accessed | tf_op | source)
XLA Modules:
  0.0 50.5 jit_solution(8508223012224998547)
XLA Ops:
  0.6 48.1 %window.1 = (f32[1,5,128,128]{3,2,1,0:T(8,128)}, f32[8]{0:T(128)}) custom-call(f32[8]{0:T(128)} %pitch_hbm.1, f32[5,5,5]{2,1,0:T(8,128)} %mixing_hbm.1, f32[1,5,128,128]{3,2,1,0:T(8,128)} %cp_hbm.1, f32[2,5,128,128]{3,2,1,0:T(8,128)} %src_hbm.1, f32[128,128]{1,0:T(8,128)} %metric_hbm.1, f32[5,128,128]{2,1,0:T(8,128)} %weight_hbm.1, f32[5,128,128]{2,1,0:T(8,128)} %end_hbm.1, ...), custom_call_target="tpu_custom_call" | custom-call | tf_op jit(solution)/shard_map/window/pallas_call | solution.py:744
  48.8 1.7 %finish.1 = (f32[1,5,128,128]{3,2,1,0:T(8,128)}, f32[8]{0:T(128)}) custom-call(f32[1,5,128,128]{3,2,1,0:T(8,128)} %get-tuple-element.4.held_hbm, f32[8]{0:T(128)} %get-tuple-element.5.grad_hbm), custom_call_target="tpu_custom_call" | custom-call | tf_op jit(solution)/shard_map/finish/pallas_call | solution.py:828

commit v5 on v4

--- a/solution.py
+++ b/solution.py
@@ -48,7 +48,7 @@
     base_ref, dd_ref, wu_ref, lift_t, sq_ref,
     p_own, p_halo, pt_own, pt_halo, pick, pick_t, pick_t2, out_buf, in_buf, back_out, back_in, y_ref, yh_ref, z_ref,
     mixed_ref, g_ref, gw_ref, gh_ref, split_ref, wf_ref, row_ref, rows_ref,
-    et_out, et_in, mg_out, mg_in, dup_out, dup_in, last_ref, turn_ref, part_ref, hint_out, hint_in, near_ref, spot_metric, spot_base,
+    et_out, et_in, mg_out, mg_in, dup_out, dup_in, last_ref, turn_ref, part_ref, hint_out, hint_in, near_ref, spot_metric, spot_base, scale_ref,
     load_sems, send_sems, recv_sems, bsend_sems, brecv_sems, hand_sems, factor_sems, gsend_sems, grecv_sems,
     table_sems, metric_sems, ghost_sems, dsend_sems, drecv_sems, round_sems, hint_sems, keep_sems,
 ):
@@ -446,10 +446,28 @@
     def lift_back():
         return dot(beside(gh_ref[k] for k in range(faces_n)), lift_ref[1:].reshape(faces_n * nodes, nodes))
 
-    def halo_part(ref, level, keep):
+    def prepare(level):
+        @pl.when(level < half)
+        def _():
+            for d in DIRS:
+                @pl.when(inside(-OFFSETS[d]))
+                def _():
+                    ghost_copy(level, d).wait_recv()
+
+            for which in range(2):
+                factor_copy(level, which).wait_recv()
+                factor_copy(level - 1, which).wait_recv()
+
+        for far in DIRS:
+            spread_metric = mg_in[far].astype(F32)
+            for c in range(comps):
+                t = in_buf[level, far, c].astype(F32)
+                scale_ref[far, c] = spread_metric * (STEP_SIZE - STEP_SIZE * t * t)
+
+    def halo_part(ref, level, slot):
         for e in range(comps):
             w = metric_ref[...] * ref[e]
-            if keep:
+            if slot is not None:
                 wf_ref[e] = w
             high = w.astype(BF16)
             split_ref[e, :blocks, :] = high
@@ -458,15 +476,25 @@
         for k in range(1, slots):
             for part in range(ghosts // chunk):
                 mix_back(k, (k - 1) * ghosts + part * chunk, chunk, part * chunk)
-        lifted = lift_back().astype(BF16)
+        lifted = lift_back()
         for d in DIRS:
             for c in range(comps):
                 row = c * ghosts + d * halo
-                back_out[level, d, c] = lifted[row : row + halo]
+                piece = lifted[row : row + halo]
+                back_out[level, d, c] = piece.astype(BF16)
+                if slot is not None:
+                    scaled = (scale_ref[d, c] * piece).astype(BF16)
+                    dup_out[slot, d, c] = scaled
+                    dup_in[slot, OFFSETS.index(-OFFSETS[d]), d, c] = scaled
         for d in DIRS:
             @pl.when(inside(-OFFSETS[d]))
             def _():
                 backward_copy(level, d).start()
+        if slot is not None:
+            for d, far in second_pairs:
+                @pl.when(inside(-OFFSETS[far]) & inside(-OFFSETS[far] - OFFSETS[d]))
+                def _():
+                    second_copy(slot, d, far).start()
 
     def own_mixing():
         for k in [*range(1, slots), 0]:
@@ -511,44 +539,15 @@
         high = levels - 1 - 2 * j
         low = high - 1
 
-        halo_part(a_ref, high, True)
-
-        @pl.when(j == 0)
-        def _():
-            for d in DIRS:
-                @pl.when(inside(-OFFSETS[d]))
-                def _():
-                    metric_copy(d).wait_recv()
-
-        @pl.when(high < half)
-        def _():
-            for d in DIRS:
-                @pl.when(inside(-OFFSETS[d]))
-                def _():
-                    ghost_copy(high, d).wait_recv()
-
-            for which in range(2):
-                factor_copy(high, which).wait_recv()
-                factor_copy(low, which).wait_recv()
-
-        for far in DIRS:
-            spread_metric = mg_in[far].astype(F32)
-            d = OFFSETS.index(-OFFSETS[far])
-            for c in range(comps):
-                t = in_buf[high, far, c].astype(F32)
-                factor = spread_metric * (STEP_SIZE - STEP_SIZE * t * t)
-                scaled = (factor * back_out[high, far, c].astype(F32)).astype(BF16)
-                dup_out[j, far, c] = scaled
-                dup_in[j, d, far, c] = scaled
-        for d, far in second_pairs:
-            @pl.when(inside(-OFFSETS[far]) & inside(-OFFSETS[far] - OFFSETS[d]))
-            def _():
-                second_copy(j, d, far).start()
-
+        halo_part(a_ref, high, j)
         add_grad(high)
         own_mixing()
         own_lift(high)
-        halo_part(base_ref, low, False)
+        halo_part(base_ref, low, None)
+
+        @pl.when(low > 0)
+        def _():
+            prepare(high - 2)
 
         @pl.when(low == 0)
         def _():
@@ -633,6 +632,12 @@
             round_step(r)
         for c in range(comps):
             a_ref[c] = a_ref[c] + weight_ref[c] * u_ref[c]
+        for d in DIRS:
+            @pl.when(inside(-OFFSETS[d]))
+            def _():
+                metric_copy(d).wait_recv()
+
+        prepare(levels - 1)
         lax.fori_loop(0, levels // 2, backward, 0)
         for c in range(comps):
             hand_copy(c).start()
@@ -802,6 +807,7 @@
             pltpu.VMEM((ghosts, faces_n * ghosts), BF16),
             pltpu.VMEM((ghosts, nodes), F32),
             pltpu.VMEM((ghosts, wide), F32),
+            pltpu.VMEM(group, F32),
             dma((10,)),
             dma((half, 4)),
             dma((half, 4)),

time: 50.7 us -> 50.4 us (level)
  no operation moved by 1% of the time
where the time goes in v5:
time: 50.4 us; the launch traced here: 50.2 us
  Pallas kernels  49.6 us (98%)
  between operations  0.64 us (1%)
    pallas_call x1, Pallas kernels, shards(): pl.pallas_call(functools.partial(window_kernel, dims), out_shape=(jax.Sha...  47.9 us
    pallas_call x1, Pallas kernels, shards(): pl.pallas_call(functools.partial(finish_kernel, comps), out_shape=(jax.Sh...  1.7 us

profile of v5, /device:TPU:1, one launch (start us, length us, event | category | flops | bytes accessed | tf_op | source)
XLA Modules:
  0.0 50.2 jit_solution(1074301106223746051)
XLA Ops:
  0.6 47.9 %window.1 = (f32[1,5,128,128]{3,2,1,0:T(8,128)}, f32[8]{0:T(128)}) custom-call(f32[8]{0:T(128)} %pitch_hbm.1, f32[5,5,5]{2,1,0:T(8,128)} %mixing_hbm.1, f32[1,5,128,128]{3,2,1,0:T(8,128)} %cp_hbm.1, f32[2,5,128,128]{3,2,1,0:T(8,128)} %src_hbm.1, f32[128,128]{1,0:T(8,128)} %metric_hbm.1, f32[5,128,128]{2,1,0:T(8,128)} %weight_hbm.1, f32[5,128,128]{2,1,0:T(8,128)} %end_hbm.1, ...), custom_call_target="tpu_custom_call" | custom-call | tf_op jit(solution)/shard_map/window/pallas_call | solution.py:749
  48.5 1.7 %finish.1 = (f32[1,5,128,128]{3,2,1,0:T(8,128)}, f32[8]{0:T(128)}) custom-call(f32[1,5,128,128]{3,2,1,0:T(8,128)} %get-tuple-element.4.held_hbm, f32[8]{0:T(128)} %get-tuple-element.5.grad_hbm), custom_call_target="tpu_custom_call" | custom-call | tf_op jit(solution)/shard_map/finish/pallas_call | solution.py:834
